TPU v7x, 32 devices: a whole 2x2x4 slice. The times are simulated.
32 devices in a mesh: cluster: 8 (over z, y), sub: 4 (over x, core).
Axes of the slice: x: 2, y: 2, z: 4, core: 2. Of those that a mesh axis runs over, the one named last changes fastest.
Arguments:
- rhs: float32 [128, 4, 384], P(('cluster', 'sub')), may hold values from -8 to 8
- operators: bfloat16 [128, 384, 384], P(('cluster', 'sub')), may hold values from -1 to 5
- signs: int32 [128, 384], P(('cluster', 'sub')), may hold values from -1 to 1, as said below
- links: int32 [128, 3, 128], P(('cluster', 'sub')), may hold values from 0 to 127, as said below
- cluster_basis: float32 [128, 24, 384], P(('cluster', 'sub')), may hold values from -0.3125 to 0.3125
- corner_basis: float32 [128, 8, 384], P(('cluster', 'sub')), may hold values from -0.3125 to 0.3125
- corner_ids: int32 [128, 8], P(('cluster', 'sub')), may hold values from 0 to 127
- cluster_coarse: float32 [8, 384, 384], P('cluster', 'sub'), may hold values from -1 to 3
- global_coarse: float32 [128, 128], P('sub'), may hold values from -0.2 to 0.5
Outputs:
- multipliers: float32 [128, 4, 384], P(('cluster', 'sub'))
- residual: float32 [128, 4, 384], P(('cluster', 'sub'))
Inputs may be any that keep to these rules, and one draw needn't show every extreme that they name: `signs`: each entry is -1 or 1. Each links[s, b] is a permutation of 0 to 127; both subdomains of an interface pair hold the same permutation for it.
All inputs are finite; a program needn't handle non-finite values.
Results may differ from a plain program's by a relative error of at most 0.007.
Values sent between devices are 32-bit elements; how exact they have to be, the bound alone decides.
A program may use at most 64 MiB of HBM per device.

v0:
```python
import functools

import jax
import jax.numpy as jnp
from jax import lax
from jax.experimental import pallas as pl
from jax.experimental.pallas import tpu as pltpu
from jax.sharding import PartitionSpec as P

ITERS = 2
LANES = 128
UNROLL = 32
MESH = pl.DeviceIdType.MESH
HIGHEST = lax.Precision.HIGHEST
NN = (((1,), (0,)), ((), ()))
NT = (((1,), (1,)), ((), ()))


def dot(a, b, dims=NN, precision=HIGHEST):
    return lax.dot_general(a, b, dims, precision=precision, preferred_element_type=jnp.float32)


def dot3(a, b, dims=NN):
    bf16, f32 = jnp.bfloat16, jnp.float32
    rows = a.shape[0]
    a_high, b_high = a.astype(bf16).astype(f32), b.astype(bf16)
    b_low = (b - b_high.astype(f32)).astype(bf16)
    halves = jnp.concatenate([a_high, a - a_high], axis=0).astype(bf16)
    out = dot(halves, b_high, dims, None)
    return out[:rows] + out[rows:] + dot(a_high.astype(bf16), b_low, dims, None)


def iota(shape, dim):
    return lax.broadcasted_iota(jnp.int32, shape, dim)


def each(count, body):
    if count <= UNROLL:
        for k in range(count):
            body(k)
    else:
        lax.fori_loop(0, count, lambda k, carry: (body(k), carry)[1], 0)


def total(ref, count, start):
    if count <= UNROLL:
        terms = [start] + [ref[k] for k in range(count)]
        while len(terms) > 1:
            terms = [sum(terms[i : i + 2][1:], terms[i]) for i in range(0, len(terms), 2)]
        return terms[0]
    return lax.fori_loop(0, count, lambda k, acc: acc + ref[k], start)


class Spread:
    def __init__(self, sizes, axes, source, slots, send, recv):
        self.sizes, self.axes = sizes, axes
        self.source, self.slots, self.send, self.recv = source, slots, send, recv
        self.count = peers_of(sizes, axes)

    def copy(self, k):
        return pltpu.make_async_remote_copy(
            src_ref=self.source,
            dst_ref=self.slots.at[k],
            send_sem=self.send.at[k],
            recv_sem=self.recv.at[k],
            device_id=peer(self.sizes, self.axes, k),
            device_id_type=MESH,
        )

    def start(self):
        each(self.count, lambda k: self.copy(k).start())

    def wait_recv(self):
        each(self.count, lambda k: self.copy(k).wait_recv())

    def wait_send(self):
        each(self.count, lambda k: self.copy(k).wait_send())


def peers_of(sizes, axes):
    clusters, members = sizes
    return {"both": clusters * members, "cluster": clusters, "sub": members}[axes] - 1


def peer(sizes, axes, k):
    clusters, members = sizes
    if axes == "both":
        c, m = (k + 1) // members, (k + 1) % members
        return {
            "cluster": lax.rem(lax.axis_index("cluster") + c, clusters),
            "sub": lax.rem(lax.axis_index("sub") + m, members),
        }
    count = clusters if axes == "cluster" else members
    return {axes: lax.rem(lax.axis_index(axes) + k + 1, count)}


def stages(sizes):
    return ("both",) if sizes[0] * sizes[1] <= UNROLL else ("cluster", "sub")


class AllSum:
    def __init__(self, sizes, refs, n):
        self.spreads = []
        for i, axes in enumerate(stages(sizes)):
            source, slots, send, recv = refs[4 * i : 4 * i + 4]
            self.spreads.append(
                Spread(sizes, axes, source.at[n], slots.at[n], send.at[n], recv.at[n])
            )

    def start(self):
        self.spreads[0].start()

    def finish(self):
        for i, spread in enumerate(self.spreads):
            spread.wait_recv()
            out = total(spread.slots, spread.count, spread.source[...])
            if i + 1 < len(self.spreads):
                self.spreads[i + 1].source[...] = out
                self.spreads[i + 1].start()
        return out

    def wait_send(self):
        for spread in self.spreads:
            spread.wait_send()


def kernel(sizes, *refs):
    clusters, members = sizes
    hbm, out_ref, refs = refs[:9], refs[9], list(refs[10:])

    def take_refs(count):
        taken = refs[:count]
        del refs[:count]
        return taken

    local_refs = take_refs(9)
    (
        rhs_ref,
        ops_ref,
        signs_ref,
        links_ref,
        cluster_basis_ref,
        corner_basis_ref,
        ids_ref,
        cluster_coarse_ref,
        global_coarse_ref,
    ) = local_refs
    (local_sem,) = take_refs(1)
    basis_ref, weights_ref, global_ref, picked_ref, swapped_basis_ref = take_refs(5)
    g_send, g_recv = take_refs(2)
    part_refs = take_refs(4)
    piece_slots, piece_send, piece_recv = take_refs(3)
    tail_refs = take_refs(4 * len(stages(sizes)))
    curve_refs = take_refs(4 * len(stages(sizes)))
    swap_refs = take_refs(8)
    table_refs = take_refs(8)

    subs, loads, dual = rhs_ref.shape
    rows = subs * loads
    kc, corn = cluster_basis_ref.shape[1], corner_basis_ref.shape[1]
    width = kc + corn
    coefs = subs * width
    order = global_coarse_ref.shape[1]
    solved = members * coefs
    my_c, my_s = lax.axis_index("cluster"), lax.axis_index("sub")
    has_low, has_high = my_s > 0, my_s < members - 1
    has_prev, has_next = my_c > 0, my_c < clusters - 1

    barrier = pltpu.get_barrier_semaphore()

    def greet(device_id):
        pl.semaphore_signal(barrier, inc=1, device_id=device_id, device_id_type=MESH)

    greeted = 0
    for axes in ("both",) if len(stages(sizes)) == 1 else ("cluster", "sub"):
        count = peers_of(sizes, axes)
        each(count, lambda k, axes=axes: greet(peer(sizes, axes, k)))
        greeted += count
    if len(stages(sizes)) > 1:
        for there, step in ((has_next, 1), (has_prev, -1)):

            @pl.when(there)
            def _():
                for m in range(1, members):
                    greet({"cluster": my_c + step, "sub": lax.rem(my_s + m, members)})

            greeted = greeted + there.astype(jnp.int32) * (members - 1)

    loads_in = [
        pltpu.make_async_copy(hbm[i], local_refs[i], local_sem.at[i]) for i in range(len(hbm))
    ]
    for i in (6, 5, 4, 0, 7, 8, 3, 2, 1):
        loads_in[i].start()
    numbers = iota((8, LANES), 1).astype(jnp.bfloat16)

    loads_in[6].wait()
    id_row = jnp.full((1, coefs), -1, jnp.int32)
    lane = iota((1, coefs), 1)
    for s in range(subs):
        for c in range(corn):
            id_row = jnp.where(lane == s * width + kc + c, ids_ref[s, c], id_row)
    id_col = jnp.sum(
        jnp.where(iota((coefs, coefs), 0) == iota((coefs, coefs), 1), id_row, 0),
        axis=1,
        keepdims=True,
    )
    weights_ref[:, solved:] = (id_col == iota((coefs, order), 1)).astype(jnp.float32)

    loads_in[5].wait()
    loads_in[4].wait()
    for s in range(subs):
        basis_ref[s * width : s * width + kc, :] = cluster_basis_ref[s]
        basis_ref[s * width + kc : (s + 1) * width, :] = corner_basis_ref[s]

    where_to = iota((1, solved), 1)
    within = lax.rem(where_to, width)
    source = (where_to // coefs) * (subs * kc) + (lax.rem(where_to, coefs) // width) * kc + within
    source = jnp.where(within < kc, source, -1)
    place = (iota((members * subs * kc, solved), 0) == source).astype(jnp.float32)
    loads_in[0].wait()
    loads_in[7].wait()
    coarse = dot(cluster_coarse_ref[0], place)
    for s in range(subs):
        weights_ref[s * width : s * width + kc, :solved] = coarse[s * kc : (s + 1) * kc]
        weights_ref[s * width + kc : (s + 1) * width, :solved] = jnp.zeros(
            (corn, solved), jnp.float32
        )

    diagonal = iota((rows, coefs), 0) // loads == iota((rows, coefs), 1) // width
    row_sub, lane_sub = iota((rows, coefs), 0) // loads, iota((rows, coefs), 1) // width
    crossed = row_sub + 1 - 2 * lax.rem(row_sub, 2) == lane_sub

    def per_load(x):
        out = x[:loads]
        for s in range(1, subs):
            out = out + x[s * loads : (s + 1) * loads]
        return out

    def lanes_added(x):
        out = x[:, :LANES]
        for b in range(1, dual // LANES):
            out = out + x[:, b * LANES : (b + 1) * LANES]
        return out

    def tiled(x):
        return jnp.concatenate([x] * subs, axis=0)

    lane_is_load = iota((loads, LANES), 0) == iota((loads, LANES), 1)

    def as_row(x):
        sums = jnp.sum(x, axis=1, keepdims=True)
        return jnp.sum(jnp.where(lane_is_load, sums, 0.0), axis=0, keepdims=True)

    def as_column(x):
        return jnp.sum(jnp.where(lane_is_load, x, 0.0), axis=1, keepdims=True)

    open_sends = []

    def piece_copy(n, side, k, step):
        target = lax.rem(my_s + k, members)
        return pltpu.make_async_remote_copy(
            src_ref=part_refs[0].at[n, target],
            dst_ref=piece_slots.at[n, side, k],
            send_sem=piece_send.at[n, side, k],
            recv_sem=piece_recv.at[n, side, k],
            device_id={"cluster": my_c + step, "sub": target},
            device_id_type=MESH,
        )

    def pieces(n, side, what):
        step = 1 - 2 * side
        for k in range(members):
            getattr(piece_copy(n, side, k, step), what)()

    def project_start(vector, n):
        raw = dot3(vector, basis_ref[...], NT)
        coef = per_load(jnp.where(diagonal, raw, 0.0))
        both = dot3(coef, weights_ref[...])
        tail_refs[0][n, :loads] = both[:, solved:]
        tail_refs[0][n, loads:, :LANES] = as_row(per_load(lanes_added(vector * vector)))
        if order > LANES:
            tail_refs[0][n, loads:, LANES:] = jnp.zeros((1, order - LANES), jnp.float32)
        for j in range(members):
            part_refs[0][n, j] = both[:, j * coefs : (j + 1) * coefs]
        tail = AllSum(sizes, tail_refs, n)
        tail.start()
        part = Spread(sizes, "sub", *[ref.at[n] for ref in part_refs])
        part.start()
        pl.when(has_next)(lambda: pieces(n, 0, "start"))
        pl.when(has_prev)(lambda: pieces(n, 1, "start"))
        return tail, part

    def project_finish(n, tail, part):
        part.wait_recv()
        pl.when(has_prev)(lambda: pieces(n, 0, "wait_recv"))
        pl.when(has_next)(lambda: pieces(n, 1, "wait_recv"))

        def cluster_of(member):
            out = part_refs[0][n, member]
            for k in range(members - 1):
                out = out + part_refs[1][n, k, member]
            return out

        def piece_sum(side):
            return total(piece_slots.at[n, side], members - 1, piece_slots[n, side, members - 1])

        own = cluster_of(my_s)
        high = cluster_of(jnp.minimum(my_s + 1, members - 1))
        low = cluster_of(jnp.maximum(my_s - 1, 0))
        prev, following = piece_sum(0), piece_sum(1)
        summed = tail.finish()
        open_sends.extend([tail, part])
        norm = as_column(summed[loads:, :LANES])
        corners = dot3(summed[:loads], picked_ref[...])

        def amount(base, i):
            return base + corners[:, i * coefs : (i + 1) * coefs]

        def block_diagonal(x, mask):
            return jnp.where(mask, tiled(x), 0.0)

        fix = dot3(block_diagonal(amount(own, 0), diagonal), basis_ref[...])
        high = jnp.where(has_high, amount(high, 1), 0.0)
        low = jnp.where(has_low, amount(low, 2), 0.0)
        following = jnp.where(has_next, amount(following, 3), 0.0)
        prev = jnp.where(has_prev, amount(prev, 4), 0.0)
        odd = lax.rem(iota((loads, coefs), 1) // width, 2) == 1
        cross = jnp.where(odd, following, prev)
        fix_swapped = jnp.concatenate(
            [
                dot3(block_diagonal(high, diagonal), swapped_basis_ref[0]),
                dot3(block_diagonal(low, diagonal), swapped_basis_ref[1]),
                dot3(block_diagonal(cross, crossed), swapped_basis_ref[2]),
            ],
            axis=1,
        )
        return fix, fix_swapped, norm

    def take(x, order_of):
        return jnp.take_along_axis(x, order_of, axis=1, mode="promise_in_bounds")

    class Swap:
        def __init__(self, refs, n):
            in_src, in_slots, in_send, in_recv, out_src, out_slots, out_send, out_recv = refs
            self.sources = [in_src.at[n, 0], in_src.at[n, 1], out_src.at[n, 0], out_src.at[n, 1]]
            self.slots = [
                in_slots.at[n, 0],
                in_slots.at[n, 1],
                out_slots.at[n, 0],
                out_slots.at[n, 1],
            ]
            self.send = [in_send.at[n, 0], in_send.at[n, 1], out_send.at[n, 0], out_send.at[n, 1]]
            self.recv = [in_recv.at[n, 0], in_recv.at[n, 1], out_recv.at[n, 0], out_recv.at[n, 1]]
            self.sends = [has_high, has_low, has_next, has_prev]
            self.takes = [has_low, has_high, has_prev, has_next]

        def copy(self, i):
            axis = "sub" if i < 2 else "cluster"
            return pltpu.make_async_remote_copy(
                src_ref=self.sources[i],
                dst_ref=self.slots[i],
                send_sem=self.send[i],
                recv_sem=self.recv[i],
                device_id={axis: lax.axis_index(axis) + (-1 if i % 2 else 1)},
                device_id_type=MESH,
            )

        def start(self, x, orders, height, extra=None):
            up_order, down_order, across_order = orders
            count = subs * height
            across = take(x[:, 2 * LANES :], across_order)
            for p in range(2):
                for h in range(subs // 2):
                    s = 2 * h + p
                    self.sources[2 + p][h * height : (h + 1) * height] = across[
                        s * height : (s + 1) * height
                    ]
            self.sources[0][:count] = take(x[:, :LANES], up_order)
            self.sources[1][:count] = take(x[:, LANES : 2 * LANES], down_order)
            if extra is not None:
                for i in range(4):
                    first = count if i < 2 else count // 2
                    self.sources[i][first : first + 8] = extra
            for i in (2, 3, 0, 1):
                pl.when(self.sends[i])(self.copy(i).start)

        def wait_recv(self):
            for i in range(4):
                pl.when(self.takes[i])(self.copy(i).wait_recv)

        def wait_send(self):
            for i in range(4):
                pl.when(self.sends[i])(self.copy(i).wait_send)

        def arrived(self, i):
            return jnp.where(self.takes[i], self.slots[i][...], 0.0)

        def field(self):
            self.wait_recv()
            at_odd, at_even = self.arrived(2), self.arrived(3)
            across = [
                (at_odd if s % 2 else at_even)[s // 2 * loads : (s // 2 + 1) * loads]
                for s in range(subs)
            ]
            return jnp.concatenate(
                [self.arrived(1), self.arrived(0), jnp.concatenate(across, axis=0)], axis=1
            )

    depth = global_coarse_ref.shape[0]
    own_rows = pl.ds(pl.multiple_of(my_s * depth, 8), depth)

    def gather_copy(k):
        return pltpu.make_async_remote_copy(
            src_ref=global_coarse_ref,
            dst_ref=global_ref.at[own_rows],
            send_sem=g_send.at[k],
            recv_sem=g_recv.at[k],
            device_id=peer(sizes, "sub", k),
            device_id_type=MESH,
        )

    def begin():
        loads_in[8].wait()
        global_ref[own_rows, :] = global_coarse_ref[...]
        each(members - 1, lambda k: gather_copy(k).start())
        loads_in[3].wait()

        def plain(row):
            return row

        def inverted(row):
            hot = (iota((LANES, LANES), 0) == row).astype(jnp.float32).astype(jnp.bfloat16)
            return dot(numbers, hot, NT, None)[:1].astype(jnp.int32)

        index = [
            [inverted(links_ref[0, s : s + 1, :]) for s in range(subs)],
            [plain(links_ref[1, s : s + 1, :]) for s in range(subs)],
            [(plain if s % 2 else inverted)(links_ref[2, s : s + 1, :]) for s in range(subs)],
        ]

        def orders_of(height):
            return [
                jnp.concatenate(
                    [jnp.broadcast_to(row, (height, LANES)) for row in block], axis=0
                )
                for block in index
            ]

        orders = orders_of(loads)
        rhs_swap = Swap(swap_refs, ITERS)
        rhs_swap.start(rhs, orders, loads)
        tables = Swap(table_refs, 0)
        ids_sent = jnp.broadcast_to(id_row.astype(jnp.float32), (8, coefs))
        tables.start(basis_ref[...], orders_of(width), width, ids_sent)

        loads_in[2].wait()
        sign = jnp.concatenate(
            [
                jnp.broadcast_to(signs_ref[s : s + 1, :].astype(jnp.float32), (loads, dual))
                for s in range(subs)
            ],
            axis=0,
        )
        each(members - 1, lambda k: gather_copy(k).wait_recv())
        tables.wait_recv()
        swapped_basis_ref[0] = tables.arrived(1)[:coefs]
        swapped_basis_ref[1] = tables.arrived(0)[:coefs]
        from_prev, from_next = tables.arrived(2), tables.arrived(3)
        for s in range(subs):
            swapped_basis_ref[2, s * width : (s + 1) * width] = (
                from_next if s % 2 else from_prev
            )[s // 2 * width : (s // 2 + 1) * width]
        id_rows = [id_row.astype(jnp.float32)]
        for i in (1, 0, 3, 2):
            first = coefs if i < 2 else coefs // 2
            id_rows.append(tables.slots[i][first : first + 1])
        whose = iota((order, coefs), 0).astype(jnp.float32)
        picks = jnp.concatenate([(row == whose).astype(jnp.float32) for row in id_rows], axis=1)
        for r in range(0, order, 2 * LANES):
            chunk = slice(r, min(r + 2 * LANES, order))
            picked_ref[chunk] = dot(global_ref[chunk], picks)
        loads_in[1].wait()
        open_sends.extend([rhs_swap, tables])
        return sign, orders, rhs_swap.field()

    rhs = jnp.concatenate([rhs_ref[s] for s in range(subs)], axis=0)
    pl.semaphore_wait(barrier, greeted)
    started = project_start(rhs, 0)
    sign, orders, residual_swapped = begin()
    fix, fix_swapped, rho = project_finish(0, *started)
    residual = rhs
    direction, direction_swapped = residual - fix, residual_swapped - fix_swapped
    row_odd = lax.rem(iota((rows, LANES), 0) // loads, 2) == 1
    there = jnp.concatenate(
        [
            jnp.full((rows, LANES), has_high.astype(jnp.float32)),
            jnp.full((rows, LANES), has_low.astype(jnp.float32)),
            jnp.where(row_odd, has_prev.astype(jnp.float32), has_next.astype(jnp.float32)),
        ],
        axis=1,
    )
    multipliers = None
    for n in range(ITERS):
        spread = sign * (direction + direction_swapped)
        spread_bf = spread.astype(jnp.bfloat16)
        image = jnp.concatenate(
            [
                dot(spread_bf[s * loads : (s + 1) * loads], ops_ref[s], NN, None)
                for s in range(subs)
            ],
            axis=0,
        )
        curve_refs[0][n] = as_row(per_load(lanes_added(spread * image)))
        curve = AllSum(sizes, curve_refs, n)
        curve.start()
        signed = sign * image
        swap = Swap(swap_refs, n)
        swap.start(signed, orders, loads)
        signed_swapped = swap.field()
        product = signed + signed_swapped
        product_swapped = signed_swapped + there * signed
        curvature = as_column(curve.finish())
        open_sends.extend([curve, swap])
        step = tiled(rho / curvature)
        residual = residual - step * product
        if n + 1 < ITERS:
            started = project_start(residual, n + 1)
        moved = step * direction
        multipliers = moved if multipliers is None else multipliers + moved
        if n + 1 < ITERS:
            residual_swapped = residual_swapped - step * product_swapped
            fix, fix_swapped, rho_new = project_finish(n + 1, *started)
            ratio = tiled(rho_new / rho)
            direction = residual - fix + ratio * direction
            direction_swapped = residual_swapped - fix_swapped + ratio * direction_swapped
            rho = rho_new
    for s in range(subs):
        out_ref[0, s] = multipliers[s * loads : (s + 1) * loads]
        out_ref[1, s] = residual[s * loads : (s + 1) * loads]
    for spread in open_sends:
        spread.wait_send()
    each(members - 1, lambda k: gather_copy(k).wait_send())
    for n in range(ITERS):
        pl.when(has_next)(lambda n=n: pieces(n, 0, "wait_send"))
        pl.when(has_prev)(lambda n=n: pieces(n, 1, "wait_send"))


def split(both_ref, mult_ref, res_ref):
    mult_ref[...] = both_ref[0]
    res_ref[...] = both_ref[1]


def local(sizes, *args):
    args = list(args)
    args[3] = jnp.transpose(args[3], (1, 0, 2))
    rhs, operators, signs, links, cluster_basis, corner_basis, ids, coarse, glob = args
    clusters, members = sizes
    subs, loads, dual = rhs.shape
    coefs = subs * (cluster_basis.shape[1] + corner_basis.shape[1])
    depth, order = glob.shape
    f32 = jnp.float32
    dma = pltpu.SemaphoreType.DMA

    def exchange(lead, block, receive):
        return [
            pltpu.VMEM(lead[:1] + block, f32),
            pltpu.VMEM(lead + receive, f32),
            dma(lead),
            dma(lead),
        ]

    def swap_scratch(count, height, extra):
        scratch = []
        for rows in (subs * height + extra, subs * height // 2 + extra):
            scratch += [
                pltpu.VMEM((count, 2, rows, LANES), f32),
                pltpu.VMEM((count, 2, rows, LANES), f32),
                dma((count, 2)),
                dma((count, 2)),
            ]
        return scratch

    def sum_scratch(block):
        scratch = []
        for axes in stages(sizes):
            scratch += exchange((ITERS, peers_of(sizes, axes)), block, block)
        return scratch

    vmem = pl.BlockSpec(memory_space=pltpu.VMEM)
    scratch = [pltpu.VMEM(a.shape, a.dtype) for a in args]
    scratch[6] = pltpu.SMEM(ids.shape, ids.dtype)
    scratch += [
        dma((len(args),)),
        pltpu.VMEM((coefs, dual), f32),
        pltpu.VMEM((coefs, members * coefs + order), f32),
        pltpu.VMEM((order, order), f32),
        pltpu.VMEM((order, 5 * coefs), f32),
        pltpu.VMEM((3, coefs, LANES), f32),
        dma((members - 1,)),
        dma((members - 1,)),
    ]
    part = (members, loads, coefs)
    scratch += exchange((ITERS, members - 1), part, part)
    scratch += [
        pltpu.VMEM((ITERS, 2, members, loads, coefs), f32),
        dma((ITERS, 2, members)),
        dma((ITERS, 2, members)),
    ]
    scratch += sum_scratch((loads + 1, order)) + sum_scratch((1, LANES))
    scratch += swap_scratch(ITERS + 1, loads, 0)
    scratch += swap_scratch(1, coefs // subs, 8)
    both = pl.pallas_call(
        functools.partial(kernel, sizes),
        out_shape=jax.ShapeDtypeStruct((2,) + rhs.shape, f32),
        in_specs=[pl.BlockSpec(memory_space=pl.ANY)] * len(args),
        out_specs=vmem,
        scratch_shapes=scratch,
        compiler_params=pltpu.CompilerParams(collective_id=0, has_side_effects=True),
    )(*args)
    return pl.pallas_call(
        split,
        out_shape=[jax.ShapeDtypeStruct(rhs.shape, f32)] * 2,
        in_specs=[vmem],
        out_specs=[vmem, vmem],
    )(both)


def solution(mesh):
    placed = (
        P(("cluster", "sub"), None, None),
        P(("cluster", "sub"), None, None),
        P(("cluster", "sub"), None),
        P(("cluster", "sub"), None, None),
        P(("cluster", "sub"), None, None),
        P(("cluster", "sub"), None, None),
        P(("cluster", "sub"), None),
        P("cluster", "sub", None),
        P("sub", None),
    )
    return jax.shard_map(
        functools.partial(local, (mesh.shape["cluster"], mesh.shape["sub"])),
        mesh=mesh,
        in_specs=placed,
        out_specs=(P(("cluster", "sub"), None, None), P(("cluster", "sub"), None, None)),
        check_vma=False,
    )
```

profile of v0, /device:TPU:0, one launch (start us, length us, event | category | flops | bytes accessed | tf_op | source)
XLA Modules:
  0.0 34.4 jit_solution(9264370232552842054)
XLA Ops:
  0.6 32.3 %shard_map.104.both_ref = f32[2,4,4,384]{3,2,1,0:T(4,128)} custom-call(f32[4,4,384]{2,1,0:T(4,128)} %refs_0_.1, bf16[4,384,384]{2,1,0:T(8,128)(2,1)} %refs_1_.1, s32[4,384]{1,0:T(4,128)} %refs_2_.1, s32[3,4,128]{2,1,0:T(4,128)} %bitcast.1, f32[4,24,384]{2,1,0:T(8,128)} %refs_4_.1, f32[4,8,384]{2,1,0:T(8,128)} %refs_5_.1, s32[4,8]{1,0:T(4,128)} %refs_6_.1, ...), custom_call_target="tpu_custom_call" | custom-call | tf_op jit(solution)/shard_map/pallas_call | solution.py:612
  33.0 1.4 %shard_map.105 = (f32[4,4,384]{2,1,0:T(4,128)}, f32[4,4,384]{2,1,0:T(4,128)}) custom-call(f32[2,4,4,384]{3,2,1,0:T(4,128)} %shard_map.104.both_ref), custom_call_target="tpu_custom_call" | custom-call | tf_op jit(solution)/shard_map/pallas_call | solution.py:620
where the time goes:
time: 34.6 us; the launch traced here: 34.4 us
  Pallas kernels  33.7 us (97%)
  between operations  0.64 us (2%)
    pallas_call x1, Pallas kernels, local(): pl.pallas_call(functools.partial(kernel, sizes), out_shape=jax.ShapeDtype...  32.3 us
    pallas_call x1, Pallas kernels, local(): pl.pallas_call(split, out_shape=[jax.ShapeDtypeStruct(rhs.shape, f32)] *...  1.42 us

commit v1 on v0

--- a/solution.py
+++ b/solution.py
@@ -282,6 +282,8 @@
             tail_refs[0][n, loads:, LANES:] = jnp.zeros((1, order - LANES), jnp.float32)
         for j in range(members):
             part_refs[0][n, j] = both[:, j * coefs : (j + 1) * coefs]
+
+    def project_send(n):
         tail = AllSum(sizes, tail_refs, n)
         tail.start()
         part = Spread(sizes, "sub", *[ref.at[n] for ref in part_refs])
@@ -484,8 +486,9 @@
         return sign, orders, rhs_swap.field()
 
     rhs = jnp.concatenate([rhs_ref[s] for s in range(subs)], axis=0)
+    project_start(rhs, 0)
     pl.semaphore_wait(barrier, greeted)
-    started = project_start(rhs, 0)
+    started = project_send(0)
     sign, orders, residual_swapped = begin()
     fix, fix_swapped, rho = project_finish(0, *started)
     residual = rhs
@@ -524,7 +527,8 @@
         step = tiled(rho / curvature)
         residual = residual - step * product
         if n + 1 < ITERS:
-            started = project_start(residual, n + 1)
+            project_start(residual, n + 1)
+            started = project_send(n + 1)
         moved = step * direction
         multipliers = moved if multipliers is None else multipliers + moved
         if n + 1 < ITERS:
@@ -545,9 +549,15 @@
         pl.when(has_prev)(lambda n=n: pieces(n, 1, "wait_send"))
 
 
-def split(both_ref, mult_ref, res_ref):
-    mult_ref[...] = both_ref[0]
-    res_ref[...] = both_ref[1]
+def split(both_ref, mult_ref, res_ref, sems):
+    copies = [
+        pltpu.make_async_copy(both_ref.at[i], out, sems.at[i])
+        for i, out in enumerate((mult_ref, res_ref))
+    ]
+    for copy in copies:
+        copy.start()
+    for copy in copies:
+        copy.wait()
 
 
 def local(sizes, *args):
@@ -611,17 +621,21 @@
     scratch += swap_scratch(1, coefs // subs, 8)
     both = pl.pallas_call(
         functools.partial(kernel, sizes),
-        out_shape=jax.ShapeDtypeStruct((2,) + rhs.shape, f32),
-        in_specs=[pl.BlockSpec(memory_space=pl.ANY)] * len(args),
+        out_shape=pltpu.VMEM((2,) + rhs.shape, f32),
+        in_specs=[pl.BlockSpec(memory_space=pltpu.HBM)] * len(args),
         out_specs=vmem,
         scratch_shapes=scratch,
-        compiler_params=pltpu.CompilerParams(collective_id=0, has_side_effects=True),
+        compiler_params=pltpu.CompilerParams(
+            collective_id=0, has_side_effects=True, vmem_limit_bytes=56 << 20
+        ),
     )(*args)
     return pl.pallas_call(
         split,
         out_shape=[jax.ShapeDtypeStruct(rhs.shape, f32)] * 2,
         in_specs=[vmem],
-        out_specs=[vmem, vmem],
+        out_specs=[pl.BlockSpec(memory_space=pltpu.HBM)] * 2,
+        scratch_shapes=[dma((2,))],
+        compiler_params=pltpu.CompilerParams(vmem_limit_bytes=4 << 20),
     )(both)
 
 

time: 34.6 us -> 32.7 us (0.945)
  Pallas kernels: 33.7 us -> 31.9 us
    pallas_call x1, Pallas kernels: 32.3 us -> 31.3 us  [local(): pl.pallas_call(functools.partial(kernel, sizes), out_shape=pltpu.VMEM((2,...]
    pallas_call x1, Pallas kernels: 1.42 us -> 0.64 us  [local(): pl.pallas_call(split, out_shape=[jax.ShapeDtypeStruct(rhs.shape, f32)] *...]
where the time goes in v1:
time: 32.7 us; the launch traced here: 32.6 us
  Pallas kernels  31.9 us (98%)
  between operations  0.64 us (2%)
    pallas_call x1, Pallas kernels, local(): pl.pallas_call(functools.partial(kernel, sizes), out_shape=pltpu.VMEM((2,...  31.3 us

profile of v1, /device:TPU:0, one launch (start us, length us, event | category | flops | bytes accessed | tf_op | source)
XLA Modules:
  0.0 32.6 jit_solution(17615991924128423949)
XLA Ops:
  0.6 31.3 %shard_map.104.both_ref = f32[2,4,4,384]{3,2,1,0:T(4,128)S(1)} custom-call(f32[4,4,384]{2,1,0:T(4,128)} %refs_0_.1, bf16[4,384,384]{2,1,0:T(8,128)(2,1)} %refs_1_.1, s32[4,384]{1,0:T(4,128)} %refs_2_.1, s32[3,4,128]{2,1,0:T(4,128)} %bitcast.1, f32[4,24,384]{2,1,0:T(8,128)} %refs_4_.1, f32[4,8,384]{2,1,0:T(8,128)} %refs_5_.1, s32[4,8]{1,0:T(4,128)} %refs_6_.1, ...), custom_call_target="tpu_custom_call" | custom-call | tf_op jit(solution)/shard_map/pallas_call | solution.py:622
  31.9 0.6 %shard_map.105 = (f32[4,4,384]{2,1,0:T(4,128)}, f32[4,4,384]{2,1,0:T(4,128)}) custom-call(f32[2,4,4,384]{3,2,1,0:T(4,128)S(1)} %shard_map.104.both_ref), custom_call_target="tpu_custom_call" | custom-call | tf_op jit(solution)/shard_map/pallas_call | solution.py:632

commit v2 on v1

--- a/solution.py
+++ b/solution.py
@@ -20,14 +20,32 @@
     return lax.dot_general(a, b, dims, precision=precision, preferred_element_type=jnp.float32)
 
 
+def halves(x):
+    high = x.astype(jnp.bfloat16)
+    return high, (x - high.astype(jnp.float32)).astype(jnp.bfloat16)
+
+
+def stacked(a):
+    high = a.astype(jnp.bfloat16).astype(jnp.float32)
+    return jnp.concatenate([high, a - high], axis=0).astype(jnp.bfloat16), high.astype(jnp.bfloat16)
+
+
+def dot2(a, b, dims=NN):
+    rows = a.shape[0]
+    out = dot(stacked(a)[0], b, dims, None)
+    return out[:rows] + out[rows:]
+
+
 def dot3(a, b, dims=NN):
-    bf16, f32 = jnp.bfloat16, jnp.float32
     rows = a.shape[0]
-    a_high, b_high = a.astype(bf16).astype(f32), b.astype(bf16)
-    b_low = (b - b_high.astype(f32)).astype(bf16)
-    halves = jnp.concatenate([a_high, a - a_high], axis=0).astype(bf16)
-    out = dot(halves, b_high, dims, None)
-    return out[:rows] + out[rows:] + dot(a_high.astype(bf16), b_low, dims, None)
+    both, high = stacked(a)
+    out = dot(both, b[0], dims, None)
+    return out[:rows] + out[rows:] + dot(high, b[1], dims, None)
+
+
+def put(ref, index, x):
+    for i, half in enumerate(halves(x)):
+        ref[(i,) + index] = half
 
 
 def iota(shape, dim):
@@ -146,10 +164,13 @@
         global_coarse_ref,
     ) = local_refs
     (local_sem,) = take_refs(1)
-    basis_ref, weights_ref, global_ref, picked_ref, swapped_basis_ref = take_refs(5)
+    basis_ref, basis_halves, swapped_basis, solve_ref, hot_ref = take_refs(5)
+    global_ref, picked_ref = take_refs(2)
     g_send, g_recv = take_refs(2)
-    part_refs = take_refs(4)
-    piece_slots, piece_send, piece_recv = take_refs(3)
+    near_coarse, near_send, near_recv = take_refs(3)
+    cross_refs = take_refs(4)
+    (share_ref,) = take_refs(1)
+    share_refs = [take_refs(3) for _ in range(2)]
     tail_refs = take_refs(4 * len(stages(sizes)))
     curve_refs = take_refs(4 * len(stages(sizes)))
     swap_refs = take_refs(8)
@@ -162,6 +183,7 @@
     coefs = subs * width
     order = global_coarse_ref.shape[1]
     solved = members * coefs
+    near = share_refs[0][0].shape[2]
     my_c, my_s = lax.axis_index("cluster"), lax.axis_index("sub")
     has_low, has_high = my_s > 0, my_s < members - 1
     has_prev, has_next = my_c > 0, my_c < clusters - 1
@@ -199,36 +221,53 @@
     for s in range(subs):
         for c in range(corn):
             id_row = jnp.where(lane == s * width + kc + c, ids_ref[s, c], id_row)
-    id_col = jnp.sum(
-        jnp.where(iota((coefs, coefs), 0) == iota((coefs, coefs), 1), id_row, 0),
-        axis=1,
-        keepdims=True,
-    )
-    weights_ref[:, solved:] = (id_col == iota((coefs, order), 1)).astype(jnp.float32)
+    whose = iota((order, coefs), 0).astype(jnp.float32)
+    corner_of = iota((coefs, order), 1).astype(jnp.float32)
+
+    def hot_of(row):
+        return (row == whose).astype(jnp.float32)
+
+    def put_hot(i, row):
+        same = iota((coefs, coefs), 0) == iota((coefs, coefs), 1)
+        column = jnp.sum(jnp.where(same, row, 0.0), axis=1, keepdims=True)
+        hot = (column == corner_of).astype(jnp.float32)
+        hot_ref[i * coefs : (i + 1) * coefs] = hot.astype(jnp.bfloat16)
+
+    put_hot(0, id_row.astype(jnp.float32))
 
     loads_in[5].wait()
     loads_in[4].wait()
     for s in range(subs):
         basis_ref[s * width : s * width + kc, :] = cluster_basis_ref[s]
         basis_ref[s * width + kc : (s + 1) * width, :] = corner_basis_ref[s]
+    put(basis_halves, (), basis_ref[...])
 
     where_to = iota((1, solved), 1)
     within = lax.rem(where_to, width)
     source = (where_to // coefs) * (subs * kc) + (lax.rem(where_to, coefs) // width) * kc + within
     source = jnp.where(within < kc, source, -1)
     place = (iota((members * subs * kc, solved), 0) == source).astype(jnp.float32)
+    place = place.astype(jnp.bfloat16)
+
+    def placed(x):
+        return [dot(half, place, NN, None).astype(jnp.bfloat16) for half in halves(x)]
+
+    solve_ref[...] = jnp.zeros(solve_ref.shape, jnp.bfloat16)
+
+    def put_solve(first, x):
+        for i, half in enumerate(placed(x)):
+            for s in range(subs):
+                at = first + s * width
+                solve_ref[i, at : at + kc] = half[s * kc : (s + 1) * kc]
+
     loads_in[0].wait()
     loads_in[7].wait()
-    coarse = dot(cluster_coarse_ref[0], place)
-    for s in range(subs):
-        weights_ref[s * width : s * width + kc, :solved] = coarse[s * kc : (s + 1) * kc]
-        weights_ref[s * width + kc : (s + 1) * width, :solved] = jnp.zeros(
-            (corn, solved), jnp.float32
-        )
+    put_solve(0, cluster_coarse_ref[0])
 
     diagonal = iota((rows, coefs), 0) // loads == iota((rows, coefs), 1) // width
     row_sub, lane_sub = iota((rows, coefs), 0) // loads, iota((rows, coefs), 1) // width
     crossed = row_sub + 1 - 2 * lax.rem(row_sub, 2) == lane_sub
+    image_sub = iota((rows, dual), 0) // loads
 
     def per_load(x):
         out = x[:loads]
@@ -245,98 +284,177 @@
     def tiled(x):
         return jnp.concatenate([x] * subs, axis=0)
 
-    lane_is_load = iota((loads, LANES), 0) == iota((loads, LANES), 1)
-
     def as_row(x):
+        shape = (x.shape[0], LANES)
         sums = jnp.sum(x, axis=1, keepdims=True)
-        return jnp.sum(jnp.where(lane_is_load, sums, 0.0), axis=0, keepdims=True)
-
-    def as_column(x):
-        return jnp.sum(jnp.where(lane_is_load, x, 0.0), axis=1, keepdims=True)
+        kept = jnp.where(iota(shape, 0) == iota(shape, 1), sums, 0.0)
+        return jnp.sum(kept, axis=0, keepdims=True)
+
+    def as_column(x, first=0):
+        mine = iota((rows, LANES), 1) == lax.rem(iota((rows, LANES), 0), loads) + first
+        return jnp.sum(jnp.where(mine, x, 0.0), axis=1, keepdims=True)
+
+    def dots(*products):
+        return as_row(jnp.concatenate([per_load(lanes_added(x)) for x in products], axis=0))
 
     open_sends = []
 
-    def piece_copy(n, side, k, step):
-        target = lax.rem(my_s + k, members)
+    def first_near(member):
+        return jnp.clip(member - 1, 0, members - near)
+
+    def near_part(ref, target):
+        return ref.at[pl.ds(first_near(target), near)]
+
+    def push(refs, at, source, step, target):
+        slots, send, recv = refs
+        device_id = {"sub": target}
+        if step:
+            device_id["cluster"] = my_c + step
         return pltpu.make_async_remote_copy(
-            src_ref=part_refs[0].at[n, target],
-            dst_ref=piece_slots.at[n, side, k],
-            send_sem=piece_send.at[n, side, k],
-            recv_sem=piece_recv.at[n, side, k],
-            device_id={"cluster": my_c + step, "sub": target},
+            src_ref=source,
+            dst_ref=slots.at[at],
+            send_sem=send.at[at],
+            recv_sem=recv.at[at],
+            device_id=device_id,
             device_id_type=MESH,
         )
 
-    def pieces(n, side, what):
-        step = 1 - 2 * side
-        for k in range(members):
-            getattr(piece_copy(n, side, k, step), what)()
-
-    def project_start(vector, n):
-        raw = dot3(vector, basis_ref[...], NT)
-        coef = per_load(jnp.where(diagonal, raw, 0.0))
-        both = dot3(coef, weights_ref[...])
-        tail_refs[0][n, :loads] = both[:, solved:]
-        tail_refs[0][n, loads:, :LANES] = as_row(per_load(lanes_added(vector * vector)))
+    class Shares:
+        def __init__(self, n):
+            own, pieces = share_refs
+            self.n = n
+            mine = share_ref.at[n]
+
+            def target(k):
+                return lax.rem(my_s + k, members)
+
+            def copies(refs, lead, of, step, ks):
+                return lambda: [
+                    push(refs, lead + (k,), of(target(k)), step, target(k)) for k in ks
+                ]
+
+            near_mine = functools.partial(near_part, mine)
+            self.groups = [(None, None, copies(own, (n,), near_mine, 0, range(1, members)))]
+            for side, sends, takes in ((0, has_next, has_prev), (1, has_prev, has_next)):
+                make = copies(
+                    pieces, (n, side), lambda t: mine.at[t], 1 - 2 * side, range(members)
+                )
+                self.groups.append((sends, takes, make))
+
+        def run(self, what):
+            for sends, takes, make in self.groups:
+                when = takes if what == "wait_recv" else sends
+
+                def act(make=make):
+                    for copy in make():
+                        getattr(copy, what)()
+
+                act() if when is None else pl.when(when)(act)
+
+        def start(self):
+            self.run("start")
+
+        def wait_send(self):
+            self.run("wait_send")
+
+        def solutions(self):
+            self.run("wait_recv")
+            n = self.n
+            own, pieces = [refs[0] for refs in share_refs]
+            base = first_near(my_s)
+
+            def sum_of(terms):
+                while len(terms) > 1:
+                    terms = [sum(terms[i : i + 2][1:], terms[i]) for i in range(0, len(terms), 2)]
+                return terms[0]
+
+            def of_member(member):
+                near_slots = [own[n, k, member - base] for k in range(1, members)]
+                return sum_of([share_ref[n, member]] + near_slots)
+
+            def of_side(side):
+                return sum_of([pieces[n, side, k] for k in range(members)])
+
+            high = of_member(jnp.minimum(my_s + 1, members - 1))
+            low = of_member(jnp.maximum(my_s - 1, 0))
+            return [of_member(my_s), high, low, of_side(1), of_side(0)]
+
+    def sums(n, raw, row):
+        tail_refs[0][n, :loads] = dot2(
+            jnp.concatenate(raw, axis=1), hot_ref[: len(raw) * coefs]
+        )
+        tail_refs[0][n, loads:, :LANES] = row
         if order > LANES:
             tail_refs[0][n, loads:, LANES:] = jnp.zeros((1, order - LANES), jnp.float32)
+        tail = AllSum(sizes, tail_refs, n)
+        share = Shares(n)
+
+        def solve():
+            share_out(n, jnp.concatenate(raw[:3], axis=1))
+
+        return tail, share, solve
+
+    def share_out(n, inside):
+        out = dot3(inside, [solve_ref[i, : inside.shape[1]] for i in range(2)])
         for j in range(members):
-            part_refs[0][n, j] = both[:, j * coefs : (j + 1) * coefs]
-
-    def project_send(n):
-        tail = AllSum(sizes, tail_refs, n)
-        tail.start()
-        part = Spread(sizes, "sub", *[ref.at[n] for ref in part_refs])
-        part.start()
-        pl.when(has_next)(lambda: pieces(n, 0, "start"))
-        pl.when(has_prev)(lambda: pieces(n, 1, "start"))
-        return tail, part
-
-    def project_finish(n, tail, part):
-        part.wait_recv()
-        pl.when(has_prev)(lambda: pieces(n, 0, "wait_recv"))
-        pl.when(has_next)(lambda: pieces(n, 1, "wait_recv"))
-
-        def cluster_of(member):
-            out = part_refs[0][n, member]
-            for k in range(members - 1):
-                out = out + part_refs[1][n, k, member]
-            return out
-
-        def piece_sum(side):
-            return total(piece_slots.at[n, side], members - 1, piece_slots[n, side, members - 1])
-
-        own = cluster_of(my_s)
-        high = cluster_of(jnp.minimum(my_s + 1, members - 1))
-        low = cluster_of(jnp.maximum(my_s - 1, 0))
-        prev, following = piece_sum(0), piece_sum(1)
+            share_ref[n, j] = out[:, j * coefs : (j + 1) * coefs]
+
+    def block_diagonal(x, mask):
+        return jnp.where(mask, tiled(x), 0.0)
+
+    def raw_of(halved, lanes, b, mask):
+        both, high = halved
+        out = dot(both[:, lanes], b[0], NT, None)
+        x = out[:rows] + out[rows:] + dot(high[:, lanes], b[1], NT, None)
+        return per_load(jnp.where(mask, x, 0.0))
+
+    def own_raw(halved):
+        return raw_of(halved, slice(0, dual), basis_halves, diagonal)
+
+    def swapped_raw(halved, i):
+        lanes = slice(i * LANES, (i + 1) * LANES)
+        b = [swapped_basis[0, i], swapped_basis[1, i]]
+        return raw_of(halved, lanes, b, crossed if i == 2 else diagonal)
+
+    def correction(tail, shares):
+        own, high, low, following, prev = shares[0].solutions()
         summed = tail.finish()
-        open_sends.extend([tail, part])
-        norm = as_column(summed[loads:, :LANES])
-        corners = dot3(summed[:loads], picked_ref[...])
+        open_sends.extend([tail] + shares)
+        corners = dot3(summed[:loads], picked_ref)
+        for share in shares[1:]:
+            late = share.solutions()
+            own, high, low, following, prev = [
+                a + b for a, b in zip((own, high, low, following, prev), late)
+            ]
 
         def amount(base, i):
             return base + corners[:, i * coefs : (i + 1) * coefs]
 
-        def block_diagonal(x, mask):
-            return jnp.where(mask, tiled(x), 0.0)
-
-        fix = dot3(block_diagonal(amount(own, 0), diagonal), basis_ref[...])
+        fix = dot3(block_diagonal(amount(own, 0), diagonal), basis_halves)
         high = jnp.where(has_high, amount(high, 1), 0.0)
         low = jnp.where(has_low, amount(low, 2), 0.0)
         following = jnp.where(has_next, amount(following, 3), 0.0)
         prev = jnp.where(has_prev, amount(prev, 4), 0.0)
         odd = lax.rem(iota((loads, coefs), 1) // width, 2) == 1
         cross = jnp.where(odd, following, prev)
+        parts = ((high, diagonal), (low, diagonal), (cross, crossed))
         fix_swapped = jnp.concatenate(
             [
-                dot3(block_diagonal(high, diagonal), swapped_basis_ref[0]),
-                dot3(block_diagonal(low, diagonal), swapped_basis_ref[1]),
-                dot3(block_diagonal(cross, crossed), swapped_basis_ref[2]),
+                dot3(block_diagonal(x, mask), [swapped_basis[0, i], swapped_basis[1, i]])
+                for i, (x, mask) in enumerate(parts)
             ],
             axis=1,
         )
-        return fix, fix_swapped, norm
+        return fix, fix_swapped, summed[loads:, :LANES]
+
+    def image_of(spread):
+        out = None
+        for s in range(subs):
+            x = dot(spread, ops_ref[s], NN, None)
+            if x.shape[0] > rows:
+                x = x[:rows] + x[rows:]
+            out = x if out is None else jnp.where(image_sub == s, x, out)
+        return out
 
     def take(x, order_of):
         return jnp.take_along_axis(x, order_of, axis=1, mode="promise_in_bounds")
@@ -367,7 +485,7 @@
                 device_id_type=MESH,
             )
 
-        def start(self, x, orders, height, extra=None):
+        def fill(self, x, orders, height, extra=None):
             up_order, down_order, across_order = orders
             count = subs * height
             across = take(x[:, 2 * LANES :], across_order)
@@ -383,6 +501,8 @@
                 for i in range(4):
                     first = count if i < 2 else count // 2
                     self.sources[i][first : first + 8] = extra
+
+        def start(self):
             for i in (2, 3, 0, 1):
                 pl.when(self.sends[i])(self.copy(i).start)
 
@@ -421,78 +541,86 @@
             device_id_type=MESH,
         )
 
-    def begin():
-        loads_in[8].wait()
-        global_ref[own_rows, :] = global_coarse_ref[...]
-        each(members - 1, lambda k: gather_copy(k).start())
-        loads_in[3].wait()
-
-        def plain(row):
-            return row
-
-        def inverted(row):
-            hot = (iota((LANES, LANES), 0) == row).astype(jnp.float32).astype(jnp.bfloat16)
-            return dot(numbers, hot, NT, None)[:1].astype(jnp.int32)
-
-        index = [
-            [inverted(links_ref[0, s : s + 1, :]) for s in range(subs)],
-            [plain(links_ref[1, s : s + 1, :]) for s in range(subs)],
-            [(plain if s % 2 else inverted)(links_ref[2, s : s + 1, :]) for s in range(subs)],
+    def near_copy(slot):
+        return pltpu.make_async_remote_copy(
+            src_ref=cluster_coarse_ref.at[0],
+            dst_ref=near_coarse.at[slot],
+            send_sem=near_send.at[slot],
+            recv_sem=near_recv.at[slot],
+            device_id={"sub": my_s + (1 if slot else -1)},
+            device_id_type=MESH,
+        )
+
+    def cross_copy(slot):
+        return pltpu.make_async_remote_copy(
+            src_ref=cross_refs[0],
+            dst_ref=cross_refs[1].at[slot],
+            send_sem=cross_refs[2].at[slot],
+            recv_sem=cross_refs[3].at[slot],
+            device_id={"cluster": my_c + (-1 if slot else 1)},
+            device_id_type=MESH,
+        )
+
+    coarse_sends = (
+        (has_low, has_high, lambda: [near_copy(0)]),
+        (has_high, has_low, lambda: [near_copy(1)]),
+    )
+
+    def coarse_run(what):
+        for sends, takes, make in coarse_sends:
+
+            def act(make=make):
+                for copy in make():
+                    getattr(copy, what)()
+
+            pl.when(takes if what == "wait_recv" else sends)(act)
+
+    def plain(row):
+        return row
+
+    def inverted(row):
+        hot = (iota((LANES, LANES), 0) == row).astype(jnp.float32).astype(jnp.bfloat16)
+        return dot(numbers, hot, NT, None)[:1].astype(jnp.int32)
+
+    loads_in[3].wait()
+    index = [
+        [inverted(links_ref[0, s : s + 1, :]) for s in range(subs)],
+        [plain(links_ref[1, s : s + 1, :]) for s in range(subs)],
+        [(plain if s % 2 else inverted)(links_ref[2, s : s + 1, :]) for s in range(subs)],
+    ]
+
+    def orders_of(height):
+        return [
+            jnp.concatenate([jnp.broadcast_to(row, (height, LANES)) for row in block], axis=0)
+            for block in index
         ]
 
-        def orders_of(height):
-            return [
-                jnp.concatenate(
-                    [jnp.broadcast_to(row, (height, LANES)) for row in block], axis=0
-                )
-                for block in index
-            ]
-
-        orders = orders_of(loads)
-        rhs_swap = Swap(swap_refs, ITERS)
-        rhs_swap.start(rhs, orders, loads)
-        tables = Swap(table_refs, 0)
-        ids_sent = jnp.broadcast_to(id_row.astype(jnp.float32), (8, coefs))
-        tables.start(basis_ref[...], orders_of(width), width, ids_sent)
-
-        loads_in[2].wait()
-        sign = jnp.concatenate(
-            [
-                jnp.broadcast_to(signs_ref[s : s + 1, :].astype(jnp.float32), (loads, dual))
-                for s in range(subs)
-            ],
-            axis=0,
-        )
-        each(members - 1, lambda k: gather_copy(k).wait_recv())
-        tables.wait_recv()
-        swapped_basis_ref[0] = tables.arrived(1)[:coefs]
-        swapped_basis_ref[1] = tables.arrived(0)[:coefs]
-        from_prev, from_next = tables.arrived(2), tables.arrived(3)
-        for s in range(subs):
-            swapped_basis_ref[2, s * width : (s + 1) * width] = (
-                from_next if s % 2 else from_prev
-            )[s // 2 * width : (s // 2 + 1) * width]
-        id_rows = [id_row.astype(jnp.float32)]
-        for i in (1, 0, 3, 2):
-            first = coefs if i < 2 else coefs // 2
-            id_rows.append(tables.slots[i][first : first + 1])
-        whose = iota((order, coefs), 0).astype(jnp.float32)
-        picks = jnp.concatenate([(row == whose).astype(jnp.float32) for row in id_rows], axis=1)
-        for r in range(0, order, 2 * LANES):
-            chunk = slice(r, min(r + 2 * LANES, order))
-            picked_ref[chunk] = dot(global_ref[chunk], picks)
-        loads_in[1].wait()
-        open_sends.extend([rhs_swap, tables])
-        return sign, orders, rhs_swap.field()
-
     rhs = jnp.concatenate([rhs_ref[s] for s in range(subs)], axis=0)
-    project_start(rhs, 0)
+    orders = orders_of(loads)
+    rhs_swap, tables = Swap(swap_refs, ITERS), Swap(table_refs, 0)
+    rhs_swap.fill(rhs, orders, loads)
+    ids_sent = jnp.broadcast_to(id_row.astype(jnp.float32), (8, coefs))
+    tables.fill(basis_ref[...], orders_of(width), width, ids_sent)
+    tail, share, solve = sums(0, [own_raw(stacked(rhs))], dots(rhs * rhs))
+    solve()
+    loads_in[8].wait()
+    global_ref[own_rows, :] = global_coarse_ref[...]
     pl.semaphore_wait(barrier, greeted)
-    started = project_send(0)
-    sign, orders, residual_swapped = begin()
-    fix, fix_swapped, rho = project_finish(0, *started)
-    residual = rhs
-    direction, direction_swapped = residual - fix, residual_swapped - fix_swapped
+    tail.start()
+    share.start()
+    tables.start()
+    each(members - 1, lambda k: gather_copy(k).start())
+    rhs_swap.start()
+    coarse_run("start")
+
+    loads_in[2].wait()
+    sign = jnp.concatenate(
+        [
+            jnp.broadcast_to(signs_ref[s : s + 1, :].astype(jnp.float32), (loads, dual))
+            for s in range(subs)
+        ],
+        axis=0,
+    )
     row_odd = lax.rem(iota((rows, LANES), 0) // loads, 2) == 1
     there = jnp.concatenate(
         [
@@ -502,51 +630,106 @@
         ],
         axis=1,
     )
-    multipliers = None
-    for n in range(ITERS):
-        spread = sign * (direction + direction_swapped)
-        spread_bf = spread.astype(jnp.bfloat16)
-        image = jnp.concatenate(
-            [
-                dot(spread_bf[s * loads : (s + 1) * loads], ops_ref[s], NN, None)
-                for s in range(subs)
-            ],
-            axis=0,
-        )
-        curve_refs[0][n] = as_row(per_load(lanes_added(spread * image)))
-        curve = AllSum(sizes, curve_refs, n)
-        curve.start()
-        signed = sign * image
-        swap = Swap(swap_refs, n)
-        swap.start(signed, orders, loads)
-        signed_swapped = swap.field()
-        product = signed + signed_swapped
-        product_swapped = signed_swapped + there * signed
-        curvature = as_column(curve.finish())
-        open_sends.extend([curve, swap])
-        step = tiled(rho / curvature)
-        residual = residual - step * product
-        if n + 1 < ITERS:
-            project_start(residual, n + 1)
-            started = project_send(n + 1)
-        moved = step * direction
-        multipliers = moved if multipliers is None else multipliers + moved
-        if n + 1 < ITERS:
-            residual_swapped = residual_swapped - step * product_swapped
-            fix, fix_swapped, rho_new = project_finish(n + 1, *started)
-            ratio = tiled(rho_new / rho)
-            direction = residual - fix + ratio * direction
-            direction_swapped = residual_swapped - fix_swapped + ratio * direction_swapped
-            rho = rho_new
+    loads_in[1].wait()
+    open_sends.extend([rhs_swap, tables])
+    each(members - 1, lambda k: gather_copy(k).wait_recv())
+    tables.wait_recv()
+    put(swapped_basis, (0,), tables.arrived(1)[:coefs])
+    put(swapped_basis, (1,), tables.arrived(0)[:coefs])
+    from_prev, from_next = tables.arrived(2), tables.arrived(3)
+    across = [
+        (from_next if s % 2 else from_prev)[s // 2 * width : (s // 2 + 1) * width]
+        for s in range(subs)
+    ]
+    put(swapped_basis, (2,), jnp.concatenate(across, axis=0))
+    id_rows = [id_row.astype(jnp.float32)]
+    for i in (1, 0, 3, 2):
+        first = coefs if i < 2 else coefs // 2
+        id_rows.append(tables.slots[i][first : first + 1])
+    picks = jnp.concatenate([hot_of(row) for row in id_rows], axis=1).astype(jnp.bfloat16)
+    for r in range(0, order, 2 * LANES):
+        chunk = slice(r, min(r + 2 * LANES, order))
+        for i, half in enumerate(halves(global_ref[chunk])):
+            picked_ref[i, chunk] = dot(half, picks, NN, None).astype(jnp.bfloat16)
+    rhs_swapped = rhs_swap.field()
+    odd = lax.rem(lane // width, 2) == 1
+    cross_ids = jnp.where(odd, id_rows[3], id_rows[4])
+    for i, row in enumerate((id_rows[1], id_rows[2], cross_ids)):
+        put_hot(i + 1, row)
+
+    coarse_run("wait_recv")
+    for slot, has in enumerate((has_high, has_low)):
+        put_solve((slot + 1) * coefs, jnp.where(has, near_coarse[slot], 0.0))
+
+    fix, fix_swapped, row = correction(tail, [share])
+    rho = as_column(row)
+    direction = rhs - fix
+    spread = sign * (direction + rhs_swapped - fix_swapped)
+    image = image_of(spread.astype(jnp.bfloat16))
+    signed = sign * image
+    halved = stacked(signed)
+    cross = swapped_raw(halved, 2)
+    cross_refs[0][...] = cross
+    pl.when(has_next)(lambda: cross_copy(0).start())
+    pl.when(has_prev)(lambda: cross_copy(1).start())
+    raw = [own_raw(halved), swapped_raw(halved, 0), swapped_raw(halved, 1), cross]
+    tail, share, solve = sums(1, raw, dots(spread * image))
+    tail.start()
+    solve()
+    share.start()
+    swap = Swap(swap_refs, 0)
+    swap.fill(signed, orders, loads)
+    swap.start()
+    pl.when(has_prev)(lambda: cross_copy(0).wait_recv())
+    pl.when(has_next)(lambda: cross_copy(1).wait_recv())
+    from_prev = jnp.where(has_prev, cross_refs[1][0], 0.0)
+    from_next = jnp.where(has_next, cross_refs[1][1], 0.0)
+    share_out(2, jnp.where(odd, from_prev, from_next))
+    late = Shares(2)
+    late.start()
+    direction_swapped = rhs_swapped - fix_swapped
+    signed_swapped = swap.field()
+    product = signed + signed_swapped
+    product_swapped = signed_swapped + there * signed
+
+    fix, fix_swapped, row = correction(tail, [share, late])
+    curvature = as_column(row)
+    step = rho / curvature
+    moved = direction - step * (product - fix)
+    moved_swapped = direction_swapped - step * (product_swapped - fix_swapped)
+    residual = rhs - step * product
+    spread_moved = sign * (moved + moved_swapped)
+    image_moved = image_of(stacked(spread_moved)[0])
+    curve_refs[0][0] = dots(
+        residual * residual,
+        spread_moved * image_moved,
+        spread_moved * image + spread * image_moved,
+    )
+    curve = AllSum(sizes, curve_refs, 0)
+    curve.start()
+    signed = sign * image_moved
+    last_swap = Swap(swap_refs, 1)
+    last_swap.fill(signed, orders, loads)
+    last_swap.start()
+    product_moved = signed + last_swap.field()
+    row = curve.finish()
+    open_sends.extend([swap, curve, last_swap])
+    ratio = as_column(row) / rho
+    last_curvature = as_column(row, loads) + ratio * (
+        as_column(row, 2 * loads) + ratio * curvature
+    )
+    last_step = ratio * rho / last_curvature
+    multipliers = (step + last_step * ratio) * direction + last_step * moved
+    residual = residual - last_step * (product_moved + ratio * product)
     for s in range(subs):
         out_ref[0, s] = multipliers[s * loads : (s + 1) * loads]
         out_ref[1, s] = residual[s * loads : (s + 1) * loads]
     for spread in open_sends:
         spread.wait_send()
     each(members - 1, lambda k: gather_copy(k).wait_send())
-    for n in range(ITERS):
-        pl.when(has_next)(lambda n=n: pieces(n, 0, "wait_send"))
-        pl.when(has_prev)(lambda n=n: pieces(n, 1, "wait_send"))
+    coarse_run("wait_send")
+    pl.when(has_next)(lambda: cross_copy(0).wait_send())
+    pl.when(has_prev)(lambda: cross_copy(1).wait_send())
 
 
 def split(both_ref, mult_ref, res_ref, sems):
@@ -590,33 +773,45 @@
             ]
         return scratch
 
-    def sum_scratch(block):
+    def sum_scratch(count, block):
         scratch = []
         for axes in stages(sizes):
-            scratch += exchange((ITERS, peers_of(sizes, axes)), block, block)
+            scratch += exchange((count, peers_of(sizes, axes)), block, block)
         return scratch
 
     vmem = pl.BlockSpec(memory_space=pltpu.VMEM)
     scratch = [pltpu.VMEM(a.shape, a.dtype) for a in args]
     scratch[6] = pltpu.SMEM(ids.shape, ids.dtype)
+    bf16 = jnp.bfloat16
+    solved = members * coefs
+    inside, columns = coarse.shape[1:]
     scratch += [
         dma((len(args),)),
         pltpu.VMEM((coefs, dual), f32),
-        pltpu.VMEM((coefs, members * coefs + order), f32),
+        pltpu.VMEM((2, coefs, dual), bf16),
+        pltpu.VMEM((2, 3, coefs, LANES), bf16),
+        pltpu.VMEM((2, 3 * coefs, solved), bf16),
+        pltpu.VMEM((4 * coefs, order), bf16),
         pltpu.VMEM((order, order), f32),
-        pltpu.VMEM((order, 5 * coefs), f32),
-        pltpu.VMEM((3, coefs, LANES), f32),
+        pltpu.VMEM((2, order, 5 * coefs), bf16),
         dma((members - 1,)),
         dma((members - 1,)),
+        pltpu.VMEM((2, inside, columns), f32),
+        dma((2,)),
+        dma((2,)),
+        pltpu.VMEM((loads, coefs), f32),
+        pltpu.VMEM((2, loads, coefs), f32),
+        dma((2,)),
+        dma((2,)),
+        pltpu.VMEM((ITERS + 1, members, loads, coefs), f32),
     ]
-    part = (members, loads, coefs)
-    scratch += exchange((ITERS, members - 1), part, part)
-    scratch += [
-        pltpu.VMEM((ITERS, 2, members, loads, coefs), f32),
-        dma((ITERS, 2, members)),
-        dma((ITERS, 2, members)),
-    ]
-    scratch += sum_scratch((loads + 1, order)) + sum_scratch((1, LANES))
+    block, near = (loads, coefs), (min(3, members), loads, coefs)
+    for lead, shape in (
+        ((ITERS + 1, members), near),
+        ((ITERS + 1, 2, members), block),
+    ):
+        scratch += [pltpu.VMEM(lead + shape, f32), dma(lead), dma(lead)]
+    scratch += sum_scratch(ITERS, (loads + 1, order)) + sum_scratch(1, (1, LANES))
     scratch += swap_scratch(ITERS + 1, loads, 0)
     scratch += swap_scratch(1, coefs // subs, 8)
     both = pl.pallas_call(

time: 32.7 us -> 29.3 us (0.90)
  Pallas kernels: 31.9 us -> 28.5 us
    pallas_call x1, Pallas kernels: 31.3 us -> 27.8 us  [local(): pl.pallas_call(functools.partial(kernel, sizes), out_shape=pltpu.VMEM((2,...]
where the time goes in v2:
time: 29.3 us; the launch traced here: 29.1 us
  Pallas kernels  28.5 us (97%)
  between operations  0.64 us (2%)
    pallas_call x1, Pallas kernels, local(): pl.pallas_call(functools.partial(kernel, sizes), out_shape=pltpu.VMEM((2,...  27.8 us
    pallas_call x1, Pallas kernels, local(): pl.pallas_call(split, out_shape=[jax.ShapeDtypeStruct(rhs.shape, f32)] *...  0.64 us

profile of v2, /device:TPU:0, one launch (start us, length us, event | category | flops | bytes accessed | tf_op | source)
XLA Modules:
  0.0 29.1 jit_solution(328128719244651334)
XLA Ops:
  0.6 27.8 %shard_map.104.both_ref = f32[2,4,4,384]{3,2,1,0:T(4,128)S(1)} custom-call(f32[4,4,384]{2,1,0:T(4,128)} %refs_0_.1, bf16[4,384,384]{2,1,0:T(8,128)(2,1)} %refs_1_.1, s32[4,384]{1,0:T(4,128)} %refs_2_.1, s32[3,4,128]{2,1,0:T(4,128)} %bitcast.1, f32[4,24,384]{2,1,0:T(8,128)} %refs_4_.1, f32[4,8,384]{2,1,0:T(8,128)} %refs_5_.1, s32[4,8]{1,0:T(4,128)} %refs_6_.1, ...), custom_call_target="tpu_custom_call" | custom-call | tf_op jit(solution)/shard_map/pallas_call | solution.py:817
  28.5 0.6 %shard_map.105 = (f32[4,4,384]{2,1,0:T(4,128)}, f32[4,4,384]{2,1,0:T(4,128)}) custom-call(f32[2,4,4,384]{3,2,1,0:T(4,128)S(1)} %shard_map.104.both_ref), custom_call_target="tpu_custom_call" | custom-call | tf_op jit(solution)/shard_map/pallas_call | solution.py:827

commit v3 on v2

--- a/solution.py
+++ b/solution.py
@@ -169,9 +169,10 @@
     g_send, g_recv = take_refs(2)
     near_coarse, near_send, near_recv = take_refs(3)
     cross_refs = take_refs(4)
+    cross_map, cross_image = take_refs(2)
     (share_ref,) = take_refs(1)
     share_refs = [take_refs(3) for _ in range(2)]
-    tail_refs = take_refs(4 * len(stages(sizes)))
+    sum_refs = [take_refs(4 * len(stages(sizes))) for _ in range(ITERS)]
     curve_refs = take_refs(4 * len(stages(sizes)))
     swap_refs = take_refs(8)
     table_refs = take_refs(8)
@@ -188,6 +189,14 @@
     has_low, has_high = my_s > 0, my_s < members - 1
     has_prev, has_next = my_c > 0, my_c < clusters - 1
 
+    def run(copies, what, there=None):
+        def act():
+            for copy in copies:
+                getattr(copy, what)()
+
+        act() if there is None else pl.when(there)(act)
+
+
     barrier = pltpu.get_barrier_semaphore()
 
     def greet(device_id):
@@ -267,7 +276,7 @@
     diagonal = iota((rows, coefs), 0) // loads == iota((rows, coefs), 1) // width
     row_sub, lane_sub = iota((rows, coefs), 0) // loads, iota((rows, coefs), 1) // width
     crossed = row_sub + 1 - 2 * lax.rem(row_sub, 2) == lane_sub
-    image_sub = iota((rows, dual), 0) // loads
+    inner, outer = slice(0, 2 * LANES), slice(2 * LANES, dual)
 
     def per_load(x):
         out = x[:loads]
@@ -329,64 +338,65 @@
                 return lax.rem(my_s + k, members)
 
             def copies(refs, lead, of, step, ks):
-                return lambda: [
-                    push(refs, lead + (k,), of(target(k)), step, target(k)) for k in ks
-                ]
+                return [push(refs, lead + (k,), of(target(k)), step, target(k)) for k in ks]
 
             near_mine = functools.partial(near_part, mine)
-            self.groups = [(None, None, copies(own, (n,), near_mine, 0, range(1, members)))]
-            for side, sends, takes in ((0, has_next, has_prev), (1, has_prev, has_next)):
-                make = copies(
-                    pieces, (n, side), lambda t: mine.at[t], 1 - 2 * side, range(members)
-                )
-                self.groups.append((sends, takes, make))
-
-        def run(self, what):
-            for sends, takes, make in self.groups:
-                when = takes if what == "wait_recv" else sends
-
-                def act(make=make):
-                    for copy in make():
-                        getattr(copy, what)()
-
-                act() if when is None else pl.when(when)(act)
+            self.near = copies(own, (n,), near_mine, 0, range(1, members))
+            self.sides = [
+                copies(pieces, (n, side), lambda t: mine.at[t], 1 - 2 * side, range(members))
+                for side in range(2)
+            ]
 
         def start(self):
-            self.run("start")
+            self.run_sides("start", has_next, has_prev)
+            run(self.near, "start")
 
         def wait_send(self):
-            self.run("wait_send")
-
-        def solutions(self):
-            self.run("wait_recv")
-            n = self.n
-            own, pieces = [refs[0] for refs in share_refs]
-            base = first_near(my_s)
-
-            def sum_of(terms):
-                while len(terms) > 1:
-                    terms = [sum(terms[i : i + 2][1:], terms[i]) for i in range(0, len(terms), 2)]
-                return terms[0]
+            self.run_sides("wait_send", has_next, has_prev)
+            run(self.near, "wait_send")
+
+        def run_sides(self, what, *theres):
+            for copies, there in zip(self.sides, theres):
+                run(copies, what, there)
+
+        def sum_of(self, terms):
+            while len(terms) > 1:
+                terms = [sum(terms[i : i + 2][1:], terms[i]) for i in range(0, len(terms), 2)]
+            return terms[0]
+
+        def of_near(self):
+            for copy in self.near:
+                copy.wait_recv()
+            slots, base = share_refs[0][0], first_near(my_s)
 
             def of_member(member):
-                near_slots = [own[n, k, member - base] for k in range(1, members)]
-                return sum_of([share_ref[n, member]] + near_slots)
-
-            def of_side(side):
-                return sum_of([pieces[n, side, k] for k in range(members)])
+                near_slots = [slots[self.n, k, member - base] for k in range(1, members)]
+                return self.sum_of([share_ref[self.n, member]] + near_slots)
 
             high = of_member(jnp.minimum(my_s + 1, members - 1))
             low = of_member(jnp.maximum(my_s - 1, 0))
-            return [of_member(my_s), high, low, of_side(1), of_side(0)]
+            return of_member(my_s), high, low
+
+        def of_sides(self):
+            self.run_sides("wait_recv", has_prev, has_next)
+            slots = share_refs[1][0]
+            prev, following = [
+                self.sum_of([slots[self.n, side, k] for k in range(members)]) for side in range(2)
+            ]
+            odd = lax.rem(iota((loads, coefs), 1) // width, 2) == 1
+            following = jnp.where(has_next, following, 0.0)
+            return jnp.where(odd, following, jnp.where(has_prev, prev, 0.0))
 
     def sums(n, raw, row):
-        tail_refs[0][n, :loads] = dot2(
+        tail_refs = sum_refs[n]
+        tail_refs[0][0, :loads] = dot2(
             jnp.concatenate(raw, axis=1), hot_ref[: len(raw) * coefs]
         )
-        tail_refs[0][n, loads:, :LANES] = row
-        if order > LANES:
-            tail_refs[0][n, loads:, LANES:] = jnp.zeros((1, order - LANES), jnp.float32)
-        tail = AllSum(sizes, tail_refs, n)
+        if row is not None:
+            tail_refs[0][0, loads:, :LANES] = row
+            if order > LANES:
+                tail_refs[0][0, loads:, LANES:] = jnp.zeros((1, order - LANES), jnp.float32)
+        tail = AllSum(sizes, tail_refs, 0)
         share = Shares(n)
 
         def solve():
@@ -411,49 +421,43 @@
     def own_raw(halved):
         return raw_of(halved, slice(0, dual), basis_halves, diagonal)
 
-    def swapped_raw(halved, i):
-        lanes = slice(i * LANES, (i + 1) * LANES)
+    def swapped_raw(halved, i, lanes):
         b = [swapped_basis[0, i], swapped_basis[1, i]]
         return raw_of(halved, lanes, b, crossed if i == 2 else diagonal)
 
-    def correction(tail, shares):
-        own, high, low, following, prev = shares[0].solutions()
+    def correction(tail, share, late=None, between=lambda: None):
+        own, high, low = share.of_near()
+        cross = share.of_sides()
         summed = tail.finish()
-        open_sends.extend([tail] + shares)
-        corners = dot3(summed[:loads], picked_ref)
-        for share in shares[1:]:
-            late = share.solutions()
-            own, high, low, following, prev = [
-                a + b for a, b in zip((own, high, low, following, prev), late)
-            ]
-
-        def amount(base, i):
-            return base + corners[:, i * coefs : (i + 1) * coefs]
-
-        fix = dot3(block_diagonal(amount(own, 0), diagonal), basis_halves)
-        high = jnp.where(has_high, amount(high, 1), 0.0)
-        low = jnp.where(has_low, amount(low, 2), 0.0)
-        following = jnp.where(has_next, amount(following, 3), 0.0)
-        prev = jnp.where(has_prev, amount(prev, 4), 0.0)
-        odd = lax.rem(iota((loads, coefs), 1) // width, 2) == 1
-        cross = jnp.where(odd, following, prev)
-        parts = ((high, diagonal), (low, diagonal), (cross, crossed))
-        fix_swapped = jnp.concatenate(
-            [
-                dot3(block_diagonal(x, mask), [swapped_basis[0, i], swapped_basis[1, i]])
-                for i, (x, mask) in enumerate(parts)
-            ],
-            axis=1,
-        )
-        return fix, fix_swapped, summed[loads:, :LANES]
-
-    def image_of(spread):
+        out = dot3(summed[:loads], picked_ref)
+        between()
+        near = [x + out[:, i * coefs : (i + 1) * coefs] for i, x in enumerate((own, high, low))]
+        open_sends.extend([tail, share])
+        if late is not None:
+            near = [x + more for x, more in zip(near, late.of_near())]
+            open_sends.append(late)
+        masked = [block_diagonal(x, diagonal) for x in near]
+        fix = dot3(masked[0], basis_halves)
+        swapped = [
+            dot3(masked[i + 1], [swapped_basis[0, i], swapped_basis[1, i]]) for i in range(2)
+        ]
+
+        def last():
+            total = cross + out[:, 3 * coefs :]
+            if late is not None:
+                total = total + late.of_sides()
+            masked = block_diagonal(total, crossed)
+            return dot3(masked, [swapped_basis[0, 2], swapped_basis[1, 2]]), masked
+
+        return fix, jnp.concatenate(swapped, axis=1), last, summed[loads:, :LANES]
+
+    def image_of(spread, depth, columns):
         out = None
         for s in range(subs):
-            x = dot(spread, ops_ref[s], NN, None)
+            x = dot(spread, ops_ref[s, depth, columns], NN, None)
             if x.shape[0] > rows:
                 x = x[:rows] + x[rows:]
-            out = x if out is None else jnp.where(image_sub == s, x, out)
+            out = x if out is None else jnp.where(iota(x.shape, 0) // loads == s, x, out)
         return out
 
     def take(x, order_of):
@@ -506,8 +510,8 @@
             for i in (2, 3, 0, 1):
                 pl.when(self.sends[i])(self.copy(i).start)
 
-        def wait_recv(self):
-            for i in range(4):
+        def wait_recv(self, which=range(4)):
+            for i in which:
                 pl.when(self.takes[i])(self.copy(i).wait_recv)
 
         def wait_send(self):
@@ -518,7 +522,6 @@
             return jnp.where(self.takes[i], self.slots[i][...], 0.0)
 
         def field(self):
-            self.wait_recv()
             at_odd, at_even = self.arrived(2), self.arrived(3)
             across = [
                 (at_odd if s % 2 else at_even)[s // 2 * loads : (s // 2 + 1) * loads]
@@ -552,28 +555,30 @@
         )
 
     def cross_copy(slot):
+        there, step = (has_prev, -1) if slot else (has_next, 1)
+        lands = jnp.where(there, slot, slot + 2)
         return pltpu.make_async_remote_copy(
             src_ref=cross_refs[0],
-            dst_ref=cross_refs[1].at[slot],
+            dst_ref=cross_refs[1].at[lands],
             send_sem=cross_refs[2].at[slot],
-            recv_sem=cross_refs[3].at[slot],
-            device_id={"cluster": my_c + (-1 if slot else 1)},
+            recv_sem=cross_refs[3].at[lands],
+            device_id={"cluster": my_c + jnp.where(there, step, -step)},
             device_id_type=MESH,
         )
 
-    coarse_sends = (
-        (has_low, has_high, lambda: [near_copy(0)]),
-        (has_high, has_low, lambda: [near_copy(1)]),
-    )
-
-    def coarse_run(what):
-        for sends, takes, make in coarse_sends:
-
-            def act(make=make):
-                for copy in make():
-                    getattr(copy, what)()
-
-            pl.when(takes if what == "wait_recv" else sends)(act)
+    def cross_wait(slot, there):
+        copy = pltpu.make_async_remote_copy(
+            src_ref=cross_refs[0],
+            dst_ref=cross_refs[1].at[slot],
+            send_sem=cross_refs[2].at[slot % 2],
+            recv_sem=cross_refs[3].at[slot],
+            device_id={"cluster": my_c},
+            device_id_type=MESH,
+        )
+        pl.when(there)(copy.wait_recv)
+
+    coarse_copies = [near_copy(0), near_copy(1)]
+    cross_copies = [cross_copy(0), cross_copy(1)]
 
     def plain(row):
         return row
@@ -601,7 +606,7 @@
     rhs_swap.fill(rhs, orders, loads)
     ids_sent = jnp.broadcast_to(id_row.astype(jnp.float32), (8, coefs))
     tables.fill(basis_ref[...], orders_of(width), width, ids_sent)
-    tail, share, solve = sums(0, [own_raw(stacked(rhs))], dots(rhs * rhs))
+    tail, share, solve = sums(0, [own_raw(stacked(rhs))], None)
     solve()
     loads_in[8].wait()
     global_ref[own_rows, :] = global_coarse_ref[...]
@@ -611,7 +616,8 @@
     tables.start()
     each(members - 1, lambda k: gather_copy(k).start())
     rhs_swap.start()
-    coarse_run("start")
+    run(coarse_copies[:1], "start", has_low)
+    run(coarse_copies[1:], "start", has_high)
 
     loads_in[2].wait()
     sign = jnp.concatenate(
@@ -633,73 +639,119 @@
     loads_in[1].wait()
     open_sends.extend([rhs_swap, tables])
     each(members - 1, lambda k: gather_copy(k).wait_recv())
-    tables.wait_recv()
+    partner = [s + 1 - 2 * (s % 2) for s in range(subs)]
+    own_ids = id_row.astype(jnp.float32)
+
+    def pick(first, id_rows):
+        picks = jnp.concatenate([hot_of(row) for row in id_rows], axis=1).astype(jnp.bfloat16)
+        lanes = slice(first * coefs, (first + len(id_rows)) * coefs)
+        for r in range(0, order, 2 * LANES):
+            chunk = slice(r, min(r + 2 * LANES, order))
+            for i, half in enumerate(halves(global_ref[chunk])):
+                picked_ref[i, chunk, lanes] = dot(half, picks, NN, None).astype(jnp.bfloat16)
+
+    tables.wait_recv(range(2))
     put(swapped_basis, (0,), tables.arrived(1)[:coefs])
     put(swapped_basis, (1,), tables.arrived(0)[:coefs])
+    id_rows = [own_ids] + [tables.slots[i][coefs : coefs + 1] for i in (1, 0)]
+    pick(0, id_rows)
+    for i in range(1, 3):
+        put_hot(i, id_rows[i])
+    rhs_swap.wait_recv(range(2))
+    tables.wait_recv(range(2, 4))
     from_prev, from_next = tables.arrived(2), tables.arrived(3)
     across = [
         (from_next if s % 2 else from_prev)[s // 2 * width : (s // 2 + 1) * width]
         for s in range(subs)
     ]
-    put(swapped_basis, (2,), jnp.concatenate(across, axis=0))
-    id_rows = [id_row.astype(jnp.float32)]
-    for i in (1, 0, 3, 2):
-        first = coefs if i < 2 else coefs // 2
-        id_rows.append(tables.slots[i][first : first + 1])
-    picks = jnp.concatenate([hot_of(row) for row in id_rows], axis=1).astype(jnp.bfloat16)
-    for r in range(0, order, 2 * LANES):
-        chunk = slice(r, min(r + 2 * LANES, order))
-        for i, half in enumerate(halves(global_ref[chunk])):
-            picked_ref[i, chunk] = dot(half, picks, NN, None).astype(jnp.bfloat16)
+    across = jnp.concatenate(across, axis=0)
+    put(swapped_basis, (2,), across)
+    odd = lax.rem(lane // width, 2) == 1
+    cross_ids = [tables.slots[i][coefs // 2 : coefs // 2 + 1] for i in (3, 2)]
+    cross_ids = jnp.where(odd, *cross_ids)
+    pick(3, [cross_ids])
+    across = across * jnp.concatenate(
+        [
+            jnp.broadcast_to(sign[loads * s : loads * s + 1, outer], (width, LANES))
+            for s in partner
+        ],
+        axis=0,
+    )
+    rhs_swap.wait_recv(range(2, 4))
     rhs_swapped = rhs_swap.field()
-    odd = lax.rem(lane // width, 2) == 1
-    cross_ids = jnp.where(odd, id_rows[3], id_rows[4])
-    for i, row in enumerate((id_rows[1], id_rows[2], cross_ids)):
-        put_hot(i + 1, row)
-
-    coarse_run("wait_recv")
+
+    def map_cross():
+        across_halves = jnp.concatenate(halves(across), axis=1)
+        out = None
+        for s in range(subs):
+            twice = jnp.concatenate([ops_ref[s, :, outer]] * 2, axis=1)
+            x = dot(twice, across_halves, NT, None)
+            out = x if out is None else jnp.where(iota(x.shape, 1) // width == partner[s], x, out)
+        for i, half in enumerate(halves(out)):
+            cross_map[:, i * coefs : (i + 1) * coefs] = half
+        put_hot(3, cross_ids)
+
+    fix, fix_swapped, last, _ = correction(tail, share, between=map_cross)
+    fix_swapped = jnp.concatenate([fix_swapped, last()[0]], axis=1)
+    direction = rhs - fix
+    direction_swapped = rhs_swapped - fix_swapped
+    spread = sign * (direction + direction_swapped)
+    spread_bf = spread.astype(jnp.bfloat16)
+    everything = slice(0, dual)
+    out = dot(spread_bf, cross_map[...], NN, None)
+    out = out[:, :coefs] + out[:, coefs:]
+    cross = per_load(jnp.where(crossed, out, 0.0))
+    image = image_of(spread_bf, everything, everything)
+    cross_refs[0][...] = cross
+    run(cross_copies, "start")
+    signed = sign * image
+    halved = stacked(signed)
+    raw = [own_raw(halved)]
+    raw += [swapped_raw(halved, i, slice(i * LANES, (i + 1) * LANES)) for i in range(2)]
+    raw.append(cross)
+    tail, share, solve = sums(1, raw, dots(spread * image, rhs * rhs))
+    tail.start()
+    run(coarse_copies[:1], "wait_recv", has_high)
+    run(coarse_copies[1:], "wait_recv", has_low)
     for slot, has in enumerate((has_high, has_low)):
         put_solve((slot + 1) * coefs, jnp.where(has, near_coarse[slot], 0.0))
-
-    fix, fix_swapped, row = correction(tail, [share])
-    rho = as_column(row)
-    direction = rhs - fix
-    spread = sign * (direction + rhs_swapped - fix_swapped)
-    image = image_of(spread.astype(jnp.bfloat16))
-    signed = sign * image
-    halved = stacked(signed)
-    cross = swapped_raw(halved, 2)
-    cross_refs[0][...] = cross
-    pl.when(has_next)(lambda: cross_copy(0).start())
-    pl.when(has_prev)(lambda: cross_copy(1).start())
-    raw = [own_raw(halved), swapped_raw(halved, 0), swapped_raw(halved, 1), cross]
-    tail, share, solve = sums(1, raw, dots(spread * image))
-    tail.start()
     solve()
     share.start()
+    for s in range(subs):
+        mine = slice(partner[s] * width, (partner[s] + 1) * width)
+        x = dot(stacked(across[mine])[0], ops_ref[s, outer, :], NN, None)
+        put(cross_image, (mine,), x[:width] + x[width:])
     swap = Swap(swap_refs, 0)
     swap.fill(signed, orders, loads)
     swap.start()
-    pl.when(has_prev)(lambda: cross_copy(0).wait_recv())
-    pl.when(has_next)(lambda: cross_copy(1).wait_recv())
+    cross_wait(0, has_prev)
+    cross_wait(1, has_next)
     from_prev = jnp.where(has_prev, cross_refs[1][0], 0.0)
     from_next = jnp.where(has_next, cross_refs[1][1], 0.0)
     share_out(2, jnp.where(odd, from_prev, from_next))
     late = Shares(2)
     late.start()
-    direction_swapped = rhs_swapped - fix_swapped
+    swap.wait_recv()
     signed_swapped = swap.field()
     product = signed + signed_swapped
     product_swapped = signed_swapped + there * signed
 
-    fix, fix_swapped, row = correction(tail, [share, late])
-    curvature = as_column(row)
+    fix, fix_swapped, last, row = correction(tail, share, late)
+    curvature, rho = as_column(row), as_column(row, loads)
     step = rho / curvature
+    residual = rhs - step * product
     moved = direction - step * (product - fix)
+
+    fix_swapped = jnp.concatenate([fix_swapped, jnp.zeros((rows, LANES), jnp.float32)], axis=1)
     moved_swapped = direction_swapped - step * (product_swapped - fix_swapped)
-    residual = rhs - step * product
     spread_moved = sign * (moved + moved_swapped)
-    image_moved = image_of(stacked(spread_moved)[0])
+    image_moved = image_of(stacked(spread_moved)[0], everything, everything)
+    last_fix, masked = last()
+    image_moved = image_moved + step * dot3(masked, cross_image)
+    last_fix = step * sign[:, outer] * last_fix
+    spread_moved = jnp.concatenate(
+        [spread_moved[:, inner], spread_moved[:, outer] + last_fix], axis=1
+    )
     curve_refs[0][0] = dots(
         residual * residual,
         spread_moved * image_moved,
@@ -711,9 +763,17 @@
     last_swap = Swap(swap_refs, 1)
     last_swap.fill(signed, orders, loads)
     last_swap.start()
+    last_swap.wait_recv()
     product_moved = signed + last_swap.field()
+    for spread in open_sends + [swap]:
+        spread.wait_send()
+    each(members - 1, lambda k: gather_copy(k).wait_send())
+    run(coarse_copies[:1], "wait_send", has_low)
+    run(coarse_copies[1:], "wait_send", has_high)
+    run(cross_copies, "wait_send")
+    cross_wait(2, my_c == clusters - 2)
+    cross_wait(3, my_c == 1)
     row = curve.finish()
-    open_sends.extend([swap, curve, last_swap])
     ratio = as_column(row) / rho
     last_curvature = as_column(row, loads) + ratio * (
         as_column(row, 2 * loads) + ratio * curvature
@@ -724,12 +784,8 @@
     for s in range(subs):
         out_ref[0, s] = multipliers[s * loads : (s + 1) * loads]
         out_ref[1, s] = residual[s * loads : (s + 1) * loads]
-    for spread in open_sends:
-        spread.wait_send()
-    each(members - 1, lambda k: gather_copy(k).wait_send())
-    coarse_run("wait_send")
-    pl.when(has_next)(lambda: cross_copy(0).wait_send())
-    pl.when(has_prev)(lambda: cross_copy(1).wait_send())
+    curve.wait_send()
+    last_swap.wait_send()
 
 
 def split(both_ref, mult_ref, res_ref, sems):
@@ -793,16 +849,18 @@
         pltpu.VMEM((2, 3 * coefs, solved), bf16),
         pltpu.VMEM((4 * coefs, order), bf16),
         pltpu.VMEM((order, order), f32),
-        pltpu.VMEM((2, order, 5 * coefs), bf16),
+        pltpu.VMEM((2, order, 4 * coefs), bf16),
         dma((members - 1,)),
         dma((members - 1,)),
         pltpu.VMEM((2, inside, columns), f32),
         dma((2,)),
         dma((2,)),
         pltpu.VMEM((loads, coefs), f32),
-        pltpu.VMEM((2, loads, coefs), f32),
+        pltpu.VMEM((4, loads, coefs), f32),
         dma((2,)),
-        dma((2,)),
+        dma((4,)),
+        pltpu.VMEM((dual, 2 * coefs), bf16),
+        pltpu.VMEM((2, coefs, dual), bf16),
         pltpu.VMEM((ITERS + 1, members, loads, coefs), f32),
     ]
     block, near = (loads, coefs), (min(3, members), loads, coefs)
@@ -811,7 +869,8 @@
         ((ITERS + 1, 2, members), block),
     ):
         scratch += [pltpu.VMEM(lead + shape, f32), dma(lead), dma(lead)]
-    scratch += sum_scratch(ITERS, (loads + 1, order)) + sum_scratch(1, (1, LANES))
+    scratch += sum_scratch(1, (loads, order)) + sum_scratch(1, (loads + 1, order))
+    scratch += sum_scratch(1, (1, LANES))
     scratch += swap_scratch(ITERS + 1, loads, 0)
     scratch += swap_scratch(1, coefs // subs, 8)
     both = pl.pallas_call(

time: 29.3 us -> 27.5 us (0.939)
  Pallas kernels: 28.5 us -> 26.7 us
    pallas_call x1, Pallas kernels: 27.8 us -> 26 us  [local(): pl.pallas_call(functools.partial(kernel, sizes), out_shape=pltpu.VMEM((2,...]
where the time goes in v3:
time: 27.5 us; the launch traced here: 27.3 us
  Pallas kernels  26.7 us (97%)
  between operations  0.64 us (2%)
    pallas_call x1, Pallas kernels, local(): pl.pallas_call(functools.partial(kernel, sizes), out_shape=pltpu.VMEM((2,...  26 us
    pallas_call x1, Pallas kernels, local(): pl.pallas_call(split, out_shape=[jax.ShapeDtypeStruct(rhs.shape, f32)] *...  0.64 us

profile of v3, /device:TPU:0, one launch (start us, length us, event | category | flops | bytes accessed | tf_op | source)
XLA Modules:
  0.0 27.3 jit_solution(1934050597647074705)
XLA Ops:
  0.6 26.0 %shard_map.104.both_ref = f32[2,4,4,384]{3,2,1,0:T(4,128)S(1)} custom-call(f32[4,4,384]{2,1,0:T(4,128)} %refs_0_.1, bf16[4,384,384]{2,1,0:T(8,128)(2,1)} %refs_1_.1, s32[4,384]{1,0:T(4,128)} %refs_2_.1, s32[3,4,128]{2,1,0:T(4,128)} %bitcast.1, f32[4,24,384]{2,1,0:T(8,128)} %refs_4_.1, f32[4,8,384]{2,1,0:T(8,128)} %refs_5_.1, s32[4,8]{1,0:T(4,128)} %refs_6_.1, ...), custom_call_target="tpu_custom_call" | custom-call | tf_op jit(solution)/shard_map/pallas_call | solution.py:876
  26.7 0.6 %shard_map.105 = (f32[4,4,384]{2,1,0:T(4,128)}, f32[4,4,384]{2,1,0:T(4,128)}) custom-call(f32[2,4,4,384]{3,2,1,0:T(4,128)S(1)} %shard_map.104.both_ref), custom_call_target="tpu_custom_call" | custom-call | tf_op jit(solution)/shard_map/pallas_call | solution.py:886

commit v4 on v3

--- a/solution.py
+++ b/solution.py
@@ -165,11 +165,12 @@
     ) = local_refs
     (local_sem,) = take_refs(1)
     basis_ref, basis_halves, swapped_basis, solve_ref, hot_ref = take_refs(5)
+    corner_rows, corner_hot = take_refs(2)
     global_ref, picked_ref = take_refs(2)
     g_send, g_recv = take_refs(2)
     near_coarse, near_send, near_recv = take_refs(3)
     cross_refs = take_refs(4)
-    cross_map, cross_image = take_refs(2)
+    (cross_image,) = take_refs(1)
     (share_ref,) = take_refs(1)
     share_refs = [take_refs(3) for _ in range(2)]
     sum_refs = [take_refs(4 * len(stages(sizes))) for _ in range(ITERS)]
@@ -236,13 +237,26 @@
     def hot_of(row):
         return (row == whose).astype(jnp.float32)
 
-    def put_hot(i, row):
+    def hot_rows(row):
         same = iota((coefs, coefs), 0) == iota((coefs, coefs), 1)
         column = jnp.sum(jnp.where(same, row, 0.0), axis=1, keepdims=True)
-        hot = (column == corner_of).astype(jnp.float32)
-        hot_ref[i * coefs : (i + 1) * coefs] = hot.astype(jnp.bfloat16)
-
-    put_hot(0, id_row.astype(jnp.float32))
+        return (column == corner_of).astype(jnp.float32)
+
+    def corners_only(x):
+        return jnp.concatenate(
+            [x[s * width + kc : (s + 1) * width] for s in range(subs)], axis=0
+        )
+
+    def put_corners(i, row, x):
+        at = slice(i * subs * corn, (i + 1) * subs * corn)
+        corner_hot[at] = corners_only(hot_rows(row)).astype(jnp.bfloat16)
+        x = corners_only(x)
+        if i > 0:
+            none = jnp.zeros(x.shape, jnp.float32)
+            x = jnp.concatenate([x if b == i - 1 else none for b in range(3)], axis=1)
+        put(corner_rows, (at,), x)
+
+    hot_ref[...] = hot_rows(id_row.astype(jnp.float32)).astype(jnp.bfloat16)
 
     loads_in[5].wait()
     loads_in[4].wait()
@@ -250,6 +264,7 @@
         basis_ref[s * width : s * width + kc, :] = cluster_basis_ref[s]
         basis_ref[s * width + kc : (s + 1) * width, :] = corner_basis_ref[s]
     put(basis_halves, (), basis_ref[...])
+    put_corners(0, id_row.astype(jnp.float32), basis_ref[...])
 
     where_to = iota((1, solved), 1)
     within = lax.rem(where_to, width)
@@ -276,6 +291,11 @@
     diagonal = iota((rows, coefs), 0) // loads == iota((rows, coefs), 1) // width
     row_sub, lane_sub = iota((rows, coefs), 0) // loads, iota((rows, coefs), 1) // width
     crossed = row_sub + 1 - 2 * lax.rem(row_sub, 2) == lane_sub
+    corner_at = iota((rows, 4 * subs * corn), 1)
+    corner_sub = lax.rem(corner_at, subs * corn) // corn
+    here = iota(corner_at.shape, 0) // loads
+    across_sub = here + 1 - 2 * lax.rem(here, 2)
+    corner_lanes = corner_sub == jnp.where(corner_at < 3 * subs * corn, here, across_sub)
     inner, outer = slice(0, 2 * LANES), slice(2 * LANES, dual)
 
     def per_load(x):
@@ -387,11 +407,9 @@
             following = jnp.where(has_next, following, 0.0)
             return jnp.where(odd, following, jnp.where(has_prev, prev, 0.0))
 
-    def sums(n, raw, row):
+    def sums(n, raw, corner_raw, hot, row):
         tail_refs = sum_refs[n]
-        tail_refs[0][0, :loads] = dot2(
-            jnp.concatenate(raw, axis=1), hot_ref[: len(raw) * coefs]
-        )
+        tail_refs[0][0, :loads] = dot2(corner_raw, hot)
         if row is not None:
             tail_refs[0][0, loads:, :LANES] = row
             if order > LANES:
@@ -400,7 +418,7 @@
         share = Shares(n)
 
         def solve():
-            share_out(n, jnp.concatenate(raw[:3], axis=1))
+            share_out(n, jnp.concatenate(raw, axis=1))
 
         return tail, share, solve
 
@@ -425,17 +443,16 @@
         b = [swapped_basis[0, i], swapped_basis[1, i]]
         return raw_of(halved, lanes, b, crossed if i == 2 else diagonal)
 
-    def correction(tail, share, late=None, between=lambda: None):
+    def correction(tail, share, late=None):
         own, high, low = share.of_near()
         cross = share.of_sides()
+        if late is not None:
+            own, high, low = [x + y for x, y in zip((own, high, low), late.of_near())]
+            open_sends.append(late)
         summed = tail.finish()
         out = dot3(summed[:loads], picked_ref)
-        between()
         near = [x + out[:, i * coefs : (i + 1) * coefs] for i, x in enumerate((own, high, low))]
         open_sends.extend([tail, share])
-        if late is not None:
-            near = [x + more for x, more in zip(near, late.of_near())]
-            open_sends.append(late)
         masked = [block_diagonal(x, diagonal) for x in near]
         fix = dot3(masked[0], basis_halves)
         swapped = [
@@ -606,16 +623,17 @@
     rhs_swap.fill(rhs, orders, loads)
     ids_sent = jnp.broadcast_to(id_row.astype(jnp.float32), (8, coefs))
     tables.fill(basis_ref[...], orders_of(width), width, ids_sent)
-    tail, share, solve = sums(0, [own_raw(stacked(rhs))], None)
+    raw = [own_raw(stacked(rhs))]
+    tail, share, solve = sums(0, raw, raw[0], hot_ref[...], None)
     solve()
     loads_in[8].wait()
     global_ref[own_rows, :] = global_coarse_ref[...]
     pl.semaphore_wait(barrier, greeted)
     tail.start()
+    tables.start()
     share.start()
-    tables.start()
+    rhs_swap.start()
     each(members - 1, lambda k: gather_copy(k).start())
-    rhs_swap.start()
     run(coarse_copies[:1], "start", has_low)
     run(coarse_copies[1:], "start", has_high)
 
@@ -651,12 +669,13 @@
                 picked_ref[i, chunk, lanes] = dot(half, picks, NN, None).astype(jnp.bfloat16)
 
     tables.wait_recv(range(2))
-    put(swapped_basis, (0,), tables.arrived(1)[:coefs])
-    put(swapped_basis, (1,), tables.arrived(0)[:coefs])
+    arrived = [tables.arrived(1)[:coefs], tables.arrived(0)[:coefs]]
+    for i in range(2):
+        put(swapped_basis, (i,), arrived[i])
     id_rows = [own_ids] + [tables.slots[i][coefs : coefs + 1] for i in (1, 0)]
     pick(0, id_rows)
     for i in range(1, 3):
-        put_hot(i, id_rows[i])
+        put_corners(i, id_rows[i], arrived[i - 1])
     rhs_swap.wait_recv(range(2))
     tables.wait_recv(range(2, 4))
     from_prev, from_next = tables.arrived(2), tables.arrived(3)
@@ -670,6 +689,7 @@
     cross_ids = [tables.slots[i][coefs // 2 : coefs // 2 + 1] for i in (3, 2)]
     cross_ids = jnp.where(odd, *cross_ids)
     pick(3, [cross_ids])
+    put_corners(3, cross_ids, across)
     across = across * jnp.concatenate(
         [
             jnp.broadcast_to(sign[loads * s : loads * s + 1, outer], (width, LANES))
@@ -680,36 +700,25 @@
     rhs_swap.wait_recv(range(2, 4))
     rhs_swapped = rhs_swap.field()
 
-    def map_cross():
-        across_halves = jnp.concatenate(halves(across), axis=1)
-        out = None
-        for s in range(subs):
-            twice = jnp.concatenate([ops_ref[s, :, outer]] * 2, axis=1)
-            x = dot(twice, across_halves, NT, None)
-            out = x if out is None else jnp.where(iota(x.shape, 1) // width == partner[s], x, out)
-        for i, half in enumerate(halves(out)):
-            cross_map[:, i * coefs : (i + 1) * coefs] = half
-        put_hot(3, cross_ids)
-
-    fix, fix_swapped, last, _ = correction(tail, share, between=map_cross)
+    fix, fix_swapped, last, _ = correction(tail, share)
     fix_swapped = jnp.concatenate([fix_swapped, last()[0]], axis=1)
     direction = rhs - fix
     direction_swapped = rhs_swapped - fix_swapped
     spread = sign * (direction + direction_swapped)
     spread_bf = spread.astype(jnp.bfloat16)
     everything = slice(0, dual)
-    out = dot(spread_bf, cross_map[...], NN, None)
-    out = out[:, :coefs] + out[:, coefs:]
-    cross = per_load(jnp.where(crossed, out, 0.0))
-    image = image_of(spread_bf, everything, everything)
+    image = image_of(spread_bf, everything, outer)
+    rest = image_of(spread_bf, everything, inner)
+    cross = swapped_raw(stacked(sign[:, outer] * image), 2, slice(0, LANES))
+    image = jnp.concatenate([rest, image], axis=1)
+    signed = sign * image
+    halved = stacked(signed)
+    corner_raw = raw_of(halved, everything, corner_rows, corner_lanes)
+    raw = [own_raw(halved)]
+    raw += [swapped_raw(halved, i, slice(i * LANES, (i + 1) * LANES)) for i in range(2)]
     cross_refs[0][...] = cross
     run(cross_copies, "start")
-    signed = sign * image
-    halved = stacked(signed)
-    raw = [own_raw(halved)]
-    raw += [swapped_raw(halved, i, slice(i * LANES, (i + 1) * LANES)) for i in range(2)]
-    raw.append(cross)
-    tail, share, solve = sums(1, raw, dots(spread * image, rhs * rhs))
+    tail, share, solve = sums(1, raw, corner_raw, corner_hot[...], dots(spread * image, rhs * rhs))
     tail.start()
     run(coarse_copies[:1], "wait_recv", has_high)
     run(coarse_copies[1:], "wait_recv", has_low)
@@ -805,7 +814,8 @@
     rhs, operators, signs, links, cluster_basis, corner_basis, ids, coarse, glob = args
     clusters, members = sizes
     subs, loads, dual = rhs.shape
-    coefs = subs * (cluster_basis.shape[1] + corner_basis.shape[1])
+    corn = corner_basis.shape[1]
+    coefs = subs * (cluster_basis.shape[1] + corn)
     depth, order = glob.shape
     f32 = jnp.float32
     dma = pltpu.SemaphoreType.DMA
@@ -847,7 +857,9 @@
         pltpu.VMEM((2, coefs, dual), bf16),
         pltpu.VMEM((2, 3, coefs, LANES), bf16),
         pltpu.VMEM((2, 3 * coefs, solved), bf16),
-        pltpu.VMEM((4 * coefs, order), bf16),
+        pltpu.VMEM((coefs, order), bf16),
+        pltpu.VMEM((2, 4 * subs * corn, dual), bf16),
+        pltpu.VMEM((4 * subs * corn, order), bf16),
         pltpu.VMEM((order, order), f32),
         pltpu.VMEM((2, order, 4 * coefs), bf16),
         dma((members - 1,)),
@@ -859,7 +871,6 @@
         pltpu.VMEM((4, loads, coefs), f32),
         dma((2,)),
         dma((4,)),
-        pltpu.VMEM((dual, 2 * coefs), bf16),
         pltpu.VMEM((2, coefs, dual), bf16),
         pltpu.VMEM((ITERS + 1, members, loads, coefs), f32),
     ]

time: 27.5 us -> 27.3 us (level)
  no operation moved by 1% of the time
where the time goes in v4:
time: 27.3 us; the launch traced here: 27.2 us
  Pallas kernels  26.5 us (97%)
  between operations  0.64 us (2%)
    pallas_call x1, Pallas kernels, local(): pl.pallas_call(functools.partial(kernel, sizes), out_shape=pltpu.VMEM((2,...  25.9 us
    pallas_call x1, Pallas kernels, local(): pl.pallas_call(split, out_shape=[jax.ShapeDtypeStruct(rhs.shape, f32)] *...  0.64 us

profile of v4, /device:TPU:0, one launch (start us, length us, event | category | flops | bytes accessed | tf_op | source)
XLA Modules:
  0.0 27.2 jit_solution(4092946350528922605)
XLA Ops:
  0.6 25.9 %shard_map.104.both_ref = f32[2,4,4,384]{3,2,1,0:T(4,128)S(1)} custom-call(f32[4,4,384]{2,1,0:T(4,128)} %refs_0_.1, bf16[4,384,384]{2,1,0:T(8,128)(2,1)} %refs_1_.1, s32[4,384]{1,0:T(4,128)} %refs_2_.1, s32[3,4,128]{2,1,0:T(4,128)} %bitcast.1, f32[4,24,384]{2,1,0:T(8,128)} %refs_4_.1, f32[4,8,384]{2,1,0:T(8,128)} %refs_5_.1, s32[4,8]{1,0:T(4,128)} %refs_6_.1, ...), custom_call_target="tpu_custom_call" | custom-call | tf_op jit(solution)/shard_map/pallas_call | solution.py:887
  26.5 0.6 %shard_map.105 = (f32[4,4,384]{2,1,0:T(4,128)}, f32[4,4,384]{2,1,0:T(4,128)}) custom-call(f32[2,4,4,384]{3,2,1,0:T(4,128)S(1)} %shard_map.104.both_ref), custom_call_target="tpu_custom_call" | custom-call | tf_op jit(solution)/shard_map/pallas_call | solution.py:897

commit v5 on v4

--- a/solution.py
+++ b/solution.py
@@ -323,8 +323,11 @@
         mine = iota((rows, LANES), 1) == lax.rem(iota((rows, LANES), 0), loads) + first
         return jnp.sum(jnp.where(mine, x, 0.0), axis=1, keepdims=True)
 
+    def summed_lanes(x):
+        return per_load(lanes_added(x)) if x.shape[0] == rows else x
+
     def dots(*products):
-        return as_row(jnp.concatenate([per_load(lanes_added(x)) for x in products], axis=0))
+        return as_row(jnp.concatenate([summed_lanes(x) for x in products], axis=0))
 
     open_sends = []
 
@@ -755,6 +758,7 @@
     moved_swapped = direction_swapped - step * (product_swapped - fix_swapped)
     spread_moved = sign * (moved + moved_swapped)
     image_moved = image_of(stacked(spread_moved)[0], everything, everything)
+    residual_lanes = summed_lanes(residual * residual)
     last_fix, masked = last()
     image_moved = image_moved + step * dot3(masked, cross_image)
     last_fix = step * sign[:, outer] * last_fix
@@ -762,7 +766,7 @@
         [spread_moved[:, inner], spread_moved[:, outer] + last_fix], axis=1
     )
     curve_refs[0][0] = dots(
-        residual * residual,
+        residual_lanes,
         spread_moved * image_moved,
         spread_moved * image + spread * image_moved,
     )

time: 27.3 us -> 27.3 us (level)
  no operation moved by 1% of the time
where the time goes in v5:
time: 27.3 us; the launch traced here: 27.2 us
  Pallas kernels  26.5 us (97%)
  between operations  0.64 us (2%)
    pallas_call x1, Pallas kernels, local(): pl.pallas_call(functools.partial(kernel, sizes), out_shape=pltpu.VMEM((2,...  25.9 us
    pallas_call x1, Pallas kernels, local(): pl.pallas_call(split, out_shape=[jax.ShapeDtypeStruct(rhs.shape, f32)] *...  0.64 us

profile of v5, /device:TPU:0, one launch (start us, length us, event | category | flops | bytes accessed | tf_op | source)
XLA Modules:
  0.0 27.2 jit_solution(2069129308101920433)
XLA Ops:
  0.6 25.9 %shard_map.104.both_ref = f32[2,4,4,384]{3,2,1,0:T(4,128)S(1)} custom-call(f32[4,4,384]{2,1,0:T(4,128)} %refs_0_.1, bf16[4,384,384]{2,1,0:T(8,128)(2,1)} %refs_1_.1, s32[4,384]{1,0:T(4,128)} %refs_2_.1, s32[3,4,128]{2,1,0:T(4,128)} %bitcast.1, f32[4,24,384]{2,1,0:T(8,128)} %refs_4_.1, f32[4,8,384]{2,1,0:T(8,128)} %refs_5_.1, s32[4,8]{1,0:T(4,128)} %refs_6_.1, ...), custom_call_target="tpu_custom_call" | custom-call | tf_op jit(solution)/shard_map/pallas_call | solution.py:891
  26.5 0.6 %shard_map.105 = (f32[4,4,384]{2,1,0:T(4,128)}, f32[4,4,384]{2,1,0:T(4,128)}) custom-call(f32[2,4,4,384]{3,2,1,0:T(4,128)S(1)} %shard_map.104.both_ref), custom_call_target="tpu_custom_call" | custom-call | tf_op jit(solution)/shard_map/pallas_call | solution.py:901
